TPU v7x, 256 devices: a whole 4x4x8 slice. The times are simulated.
256 devices in a mesh: member: 16 (over z_hi, y), lat: 4 (over z_lo, core), lon: 4 (over x).
Axes of the slice: x: 4, y: 4, z: 8 (z_hi: 4, z_lo: 2; z = z_hi * 2 + z_lo), core: 2. Of those that a mesh axis runs over, the one named last changes fastest.
Arguments:
- layer_inputs: bfloat16 [16, 256, 192, 512], P('member', None, 'lat', 'lon'), may hold values from -6 to 6
- conv_weight: bfloat16 [3, 3, 69, 256], replicated, may hold values from -0.125 to 0.125
- channel_offset: float32 [69], replicated, may hold values from -4 to 4
- observed: bfloat16 [69, 192, 512], P(None, 'lat', 'lon'), may hold values from -6 to 6
- var_weight: float32 [69], replicated, may hold values from 0.5 to 4
Outputs:
- predicted_fields: bfloat16 [16, 69, 192, 512], P('member', None, 'lat', 'lon')
- input_slope_field: bfloat16 [16, 256, 192, 512], P('member', None, 'lat', 'lon')
All inputs are finite; a program needn't handle non-finite values.
Results may differ from a plain program's by a relative error of at most 0.0063.
Values may be sent and summed in bfloat16 or wider, within the bound.
A program may use at most 192 MiB of HBM per device.

v0:
```python
import jax
import jax.numpy as jnp
from jax import lax
from jax.sharding import PartitionSpec as P

smoothing = 0.25


def extended(shard, sides, width, wrap):
    for axis, dim in sides:
        size, length = (lax.axis_size(axis), shard.shape[dim])
        up = [(i, (i + 1) % size) for i in range(size if wrap else size - 1)]
        down = [(j, i) for i, j in up]
        last = lax.slice_in_dim(shard, length - width, length, axis=dim)
        initial = lax.slice_in_dim(shard, 0, width, axis=dim)
        before = lax.ppermute(last, axis, up)
        after = lax.ppermute(initial, axis, down)
        shard = jnp.concatenate([before, shard, after], axis=dim)
    return shard


def smooth(difference):
    return difference * lax.rsqrt(difference * difference + smoothing * smoothing)


def extend(field):
    widened = extended(field, (("lon", 3),), 1, True)
    return extended(widened, (("lat", 2),), 1, False)


def pair_total(quantity_table, others):

    def add_member(member_index, running):
        member_values = lax.dynamic_index_in_dim(others, member_index, 0, keepdims=True).astype(
            jnp.float32
        )
        return running + smooth(quantity_table - member_values)

    return lax.fori_loop(
        0,
        others.shape[0],
        add_member,
        jnp.zeros(
            quantity_table.shape[:0] + (others.shape[0],) + quantity_table.shape[1:], jnp.float32
        ),
    )


def latitude_weight(first_row, count, total_rows):
    row_index = (first_row + jnp.arange(count)).astype(jnp.float32)
    return jnp.cos((-80.0 + 160.0 * (row_index + 0.5) / float(total_rows)) * (jnp.pi / 180.0))


def shards(layer_inputs, conv_weight, channel_offset, observed, var_weight):
    tile_rows = layer_inputs.shape[2]
    tile_cols = layer_inputs.shape[3]
    channels = layer_inputs.shape[1]
    outputs = conv_weight.shape[2]
    members = lax.axis_size("member")
    total_rows = tile_rows * lax.axis_size("lat")
    padded = extend(layer_inputs)[0]
    accumulated_outcome = jnp.zeros((outputs, tile_rows, tile_cols), jnp.float32)
    for row_tap in range(3):
        for col_tap in range(3):
            window = padded[:, row_tap : row_tap + tile_rows, col_tap : col_tap + tile_cols]
            accumulated_outcome = accumulated_outcome + lax.dot_general(
                conv_weight[row_tap, col_tap],
                window,
                (((1,), (0,)), ((), ())),
                preferred_element_type=jnp.float32,
            )
    predicted_fields = (accumulated_outcome + channel_offset[:, None, None]).astype(jnp.bfloat16)[
        None
    ]
    slice_rows = tile_rows // members
    slice_start = lax.axis_index("member") * slice_rows
    obs_slice = (
        lax.dynamic_slice_in_dim(observed, slice_start, slice_rows, 1)
        .astype(jnp.float32)
        .reshape(outputs, slice_rows * tile_cols)
    )
    slice_lat = latitude_weight(
        lax.axis_index("lat") * tile_rows + slice_start, slice_rows, total_rows
    )
    labels = jnp.broadcast_to(
        jnp.arange(outputs).astype(jnp.bfloat16)[None, :, None, None], (1, outputs, members, 128)
    )
    member_block = lax.all_to_all(
        predicted_fields, "member", split_axis=2, concat_axis=0, tiled=True
    )
    label_block = lax.all_to_all(labels, "member", split_axis=2, concat_axis=0, tiled=True)
    quantity_table = member_block.astype(jnp.float32)
    pair_block = pair_total(quantity_table, member_block)
    picked = label_block[0, :, 0, 0].astype(jnp.float32)
    selector = (picked[:, None] == jnp.arange(outputs).astype(jnp.float32)[None, :]).astype(
        jnp.float32
    )
    target = jnp.dot(selector, obs_slice, precision=lax.Precision.HIGHEST).reshape(
        picked.shape[0], slice_rows, tile_cols
    )[None]
    weights = jnp.dot(selector, var_weight, precision=lax.Precision.HIGHEST)
    grad_block = (
        slice_lat[:, None]
        * weights[:, None, None]
        * (smooth(quantity_table - target) - pair_block / (members - 1))
    ).astype(jnp.bfloat16)
    gradient = lax.all_to_all(grad_block, "member", split_axis=0, concat_axis=2, tiled=True)
    grad_padded = extend(gradient)[0]
    reverse_aggregate = jnp.zeros((channels, tile_rows, tile_cols), jnp.float32)
    for row_tap in range(3):
        for col_tap in range(3):
            window = grad_padded[
                :, 2 - row_tap : 2 - row_tap + tile_rows, 2 - col_tap : 2 - col_tap + tile_cols
            ]
            reverse_aggregate = reverse_aggregate + lax.dot_general(
                conv_weight[row_tap, col_tap],
                window,
                (((0,), (0,)), ((), ())),
                preferred_element_type=jnp.float32,
            )
    return (predicted_fields, reverse_aggregate.astype(jnp.bfloat16)[None])


def solution(mesh):
    in_specs = (P("member", None, "lat", "lon"), P(), P(), P(None, "lat", "lon"), P())
    out_specs = (P("member", None, "lat", "lon"), P("member", None, "lat", "lon"))
    return jax.shard_map(shards, mesh=mesh, in_specs=in_specs, out_specs=out_specs, check_vma=False)
```

profile of v0, /device:TPU:1, one launch (start us, length us, event | category | flops | bytes accessed | tf_op | source)
XLA Modules:
  0.0 282.5 jit_solution(7492653918290534328)
XLA Ops:
  0.6 7.0 %fusion.90 = (bf16[1,256,48,1]{3,2,1,0:T(8,128)(2,1)}, bf16[1,256,48,1]{3,2,1,0:T(8,128)(2,1)}) fusion(bf16[1,256,48,128]{3,2,1,0:T(8,128)(2,1)} %param.7), kind=kLoop, calls=%fused_computation.107 | loop fusion | bytes 98304 | tf_op jit(solution)/shard_map/slice | solution.py:14
  7.6 4.5 %copy.57 = bf16[1,256,48,1]{1,2,3,0:T(8,128)(2,1)S(1)} copy(bf16[1,256,48,1]{3,2,1,0:T(8,128)(2,1)} %get-tuple-element.123) | data formatting | bytes 49152
  14.3 4.5 %copy.58 = bf16[1,256,48,1]{1,2,3,0:T(8,128)(2,1)S(1)} copy(bf16[1,256,48,1]{3,2,1,0:T(8,128)(2,1)} %get-tuple-element.124) | data formatting | bytes 49152
  20.2 4.3 %copy.43 = bf16[1,256,48,128]{3,1,2,0:T(8,128)(2,1)} copy(bf16[1,256,48,128]{3,2,1,0:T(8,128)(2,1)} %param.7) | data formatting | bytes 6291456 | tf_op args[0]
  31.2 4.8 %collective-permute-start.2 = (bf16[1,256,1,130]{3,1,2,0:T(8,128)(2,1)S(1)}, bf16[1,256,1,130]{3,1,2,0:T(8,128)(2,1)S(1)}, u32[]{:S(2)}, u32[]{:S(2)}) collective-permute-start(bf16[1,256,1,130]{3,1,2,0:T(8,128)(2,1)S(1)} %get-tuple-element.121), channel_id=1, source_target_pairs={{0,4},{4,8},{8,12},{1,5},{5,9},{9,13},{2,6},{6,10},{10,14},{3,7},{... | collective-permute-start | bytes 199688 | tf_op jit(solution)/shard_map/ppermute | solution.py:16
  38.8 10.3 %all-to-all-start = ((bf16[1,69,16,128]{3,1,0,2:T(8,128)(2,1)}), bf16[1,69,16,128]{3,1,0,2:T(8,128)(2,1)S(1)}, u32[]{:S(2)}, u32[]{:S(2)}) async-start(bf16[1,69,16,128]{3,1,0,2:T(8,128)(2,1)} %broadcast_in_dim.9), calls=%async_computation | async-start | bytes 589824 | tf_op jit(solution)/shard_map/all_to_all | solution.py:91
  49.2 6.6 %maximum_bitcast_fusion = bf16[256,50,130]{2,0,1:T(8,128)(2,1)S(1)} fusion(bf16[1,256,1,130]{3,1,2,0:T(8,128)(2,1)S(1)} %collective-permute-done.3, bf16[1,256,48,1]{3,1,2,0:T(8,128)(2,1)} %copy.44, bf16[1,256,48,128]{3,1,2,0:T(8,128)(2,1)} %copy.43, bf16[1,256,48,1]{3,1,2,0:T(8,128)(2,1)} %copy.42, bf16[1,256,1,130]{3,1,2,0:T(8,128)(2,1)S(1)} %collective-permute-done.2), kind=kLoop, calls=%fused_computation.4 | loop fusion | flops 16640000 | bytes 6656000 | tf_op jit(solution)/shard_map/squeeze | solution.py:61
  66.5 21.8 %all-to-all-start.1 = ((bf16[1,69,48,128]{3,1,0,2:T(8,128)(2,1)}), bf16[1,69,48,128]{3,1,0,2:T(8,128)(2,1)}, u32[]{:S(2)}, u32[]{:S(2)}) async-start(bf16[1,69,48,128]{3,1,0,2:T(8,128)(2,1)} %bitcast.27), calls=%async_computation.1 | async-start | bytes 1769472 | tf_op jit(solution)/shard_map/all_to_all | solution.py:88
  89.3 24.2 %all-to-all-done.1 = bf16[1,69,48,128]{3,1,0,2:T(8,128)(2,1)} async-done(((bf16[1,69,48,128]{3,1,0,2:T(8,128)(2,1)}), bf16[1,69,48,128]{3,1,0,2:T(8,128)(2,1)}, u32[]{:S(2)}, u32[]{:S(2)}) %all-to-all-start.1) | async-done | bytes 847904 | tf_op jit(solution)/shard_map/all_to_all | solution.py:88
  113.5 3.0 %copy.48 = f32[16,69,3,128]{3,2,1,0:T(4,128)} copy(bf16[16,69,3,128]{3,1,2,0:T(8,128)(2,1)} %bitcast.30) | data formatting | bytes 2543616
  116.5 60.7 %while.14 = (s32[]{:T(128)}, f32[16,69,3,128]{3,2,1,0:T(4,128)S(1)}, bf16[16,69,3,128]{3,1,2,0:T(8,128)(2,1)}, f32[16,69,3,128]{3,2,1,0:T(4,128)}, s32[]{:T(128)}, /*index=5*/s32[]{:T(128)}) while((s32[]{:T(128)}, f32[16,69,3,128]{3,2,1,0:T(4,128)S(1)}, bf16[16,69,3,128]{3,1,2,0:T(8,128)(2,1)}, f32[16,69,3,128]{3,2,1,0:T(4,128)}, ...), condition=%wide.region_1.2_spmd.clone, body=%wide.region_0.1_spmd.clone.sunk | while | flops 2570115 | bytes 5458267 | solution.py:39
  124.9 2.9 %select_add_fusion.2 = f32[16,69,3,128]{3,2,1,0:T(4,128)S(1)} fusion(f32[16,69,3,128]{3,2,1,0:T(4,128)S(1)} %get-tuple-element.161, f32[16,69,3,128]{3,2,1,0:T(4,128)} %get-tuple-element.169, f32[69,3,128]{2,1,0:T(4,128)S(1)} %fusion.93, pred[]{:T(512)S(6)} %compare.3), kind=kLoop, calls=%fused_computation.clone.1 | loop fusion | flops 2543616 | bytes 5193217 | tf_op jit(solution)/shard_map/while/body/eval_jaxpr/add | solution.py:37
  128.7 2.9 %select_add_fusion.2 = f32[16,69,3,128]{3,2,1,0:T(4,128)S(1)} fusion(f32[16,69,3,128]{3,2,1,0:T(4,128)S(1)} %get-tuple-element.161, f32[16,69,3,128]{3,2,1,0:T(4,128)} %get-tuple-element.169, f32[69,3,128]{2,1,0:T(4,128)S(1)} %fusion.93, pred[]{:T(512)S(6)} %compare.3), kind=kLoop, calls=%fused_computation.clone.1 | loop fusion | flops 2543616 | bytes 5193217 | tf_op jit(solution)/shard_map/while/body/eval_jaxpr/add | solution.py:37
  178.9 29.9 %all_to_all.54 = bf16[16,69,3,128]{3,1,2,0:T(8,128)(2,1)S(1)} all-to-all(bf16[16,69,3,128]{3,1,2,0:T(8,128)(2,1)S(1)} %fusion.22), channel_id=1, replica_groups=mesh['member'=16,'lat'=4,'lon'=4] {'member'}, dimensions={0} | all-to-all | bytes 1695744 | tf_op jit(solution)/shard_map/all_to_all | solution.py:107
  224.5 4.5 %fusion.24 = f32[48,128,256]{2,1,0:T(8,128)} fusion(bf16[69,50,130]{2,0,1:T(8,128)(2,1)S(1)} %maximum_bitcast_fusion.1, bf16[3,3,69,256]{3,2,1,0:T(8,128)(2,1)S(1)} %copy-done.6), kind=kOutput, calls=%fused_computation.33 | convolution fusion | flops 217055232 | bytes 7213056 | tf_op jit(solution)/shard_map/dot_general | solution.py:115
  229.0 4.5 %fusion.26 = f32[48,128,256]{2,1,0:T(8,128)} fusion(bf16[69,50,130]{2,0,1:T(8,128)(2,1)S(1)} %maximum_bitcast_fusion.1, bf16[3,3,69,256]{3,2,1,0:T(8,128)(2,1)S(1)} %copy-done.6), kind=kOutput, calls=%fused_computation.35 | convolution fusion | flops 217055232 | bytes 7213056 | tf_op jit(solution)/shard_map/dot_general | solution.py:115
  233.5 3.6 %fusion.28 = f32[48,128,256]{2,1,0:T(8,128)} fusion(bf16[69,50,130]{2,0,1:T(8,128)(2,1)S(1)} %maximum_bitcast_fusion.1, bf16[3,3,69,256]{3,2,1,0:T(8,128)(2,1)S(1)} %copy-done.6), kind=kOutput, calls=%fused_computation.37 | convolution fusion | flops 217055232 | bytes 7213056 | tf_op jit(solution)/shard_map/dot_general | solution.py:115
  237.1 4.5 %fusion.30 = f32[48,128,256]{2,1,0:T(8,128)} fusion(bf16[69,50,130]{2,0,1:T(8,128)(2,1)S(1)} %maximum_bitcast_fusion.1, bf16[3,3,69,256]{3,2,1,0:T(8,128)(2,1)S(1)} %copy-done.6), kind=kOutput, calls=%fused_computation.39 | convolution fusion | flops 217055232 | bytes 7213056 | tf_op jit(solution)/shard_map/dot_general | solution.py:115
  241.6 4.6 %fusion.32 = f32[48,128,256]{2,1,0:T(8,128)} fusion(bf16[69,50,130]{2,0,1:T(8,128)(2,1)S(1)} %maximum_bitcast_fusion.1, bf16[3,3,69,256]{3,2,1,0:T(8,128)(2,1)S(1)} %copy-done.6), kind=kOutput, calls=%fused_computation.41 | convolution fusion | flops 217055232 | bytes 7213056 | tf_op jit(solution)/shard_map/dot_general | solution.py:115
  246.2 3.8 %fusion.34 = f32[48,128,256]{2,1,0:T(8,128)} fusion(bf16[69,50,130]{2,0,1:T(8,128)(2,1)S(1)} %maximum_bitcast_fusion.1, bf16[3,3,69,256]{3,2,1,0:T(8,128)(2,1)S(1)} %copy-done.6), kind=kOutput, calls=%fused_computation.43 | convolution fusion | flops 217055232 | bytes 7213056 | tf_op jit(solution)/shard_map/dot_general | solution.py:115
  249.9 4.5 %fusion.36 = f32[48,128,256]{2,1,0:T(8,128)} fusion(bf16[69,50,130]{2,0,1:T(8,128)(2,1)S(1)} %maximum_bitcast_fusion.1, bf16[3,3,69,256]{3,2,1,0:T(8,128)(2,1)S(1)} %copy-done.6), kind=kOutput, calls=%fused_computation.45 | convolution fusion | flops 217055232 | bytes 7213056 | tf_op jit(solution)/shard_map/dot_general | solution.py:115
  254.4 4.5 %fusion.38 = f32[48,128,256]{2,1,0:T(8,128)} fusion(bf16[69,50,130]{2,0,1:T(8,128)(2,1)S(1)} %maximum_bitcast_fusion.1, bf16[3,3,69,256]{3,2,1,0:T(8,128)(2,1)S(1)} %copy-done.6), kind=kOutput, calls=%fused_computation.47 | convolution fusion | flops 217055232 | bytes 7213056 | tf_op jit(solution)/shard_map/dot_general | solution.py:115
  258.9 18.5 %fusion.1 = bf16[1,256,48,128]{1,3,2,0:T(8,128)(2,1)} fusion(f32[48,128,256]{2,1,0:T(8,128)} %fusion.24, f32[48,128,256]{2,1,0:T(8,128)} %fusion.26, f32[48,128,256]{2,1,0:T(8,128)} %fusion.28, f32[48,128,256]{2,1,0:T(8,128)} %fusion.30, f32[48,128,256]{2,1,0:T(8,128)} %fusion.32, f32[48,128,256]{2,1,0:T(8,128)} %fusion.34, f32[48,128,256]{2,1,0:T(8,128)} %fusion.38, ...), kind=kOutput, calls=%fused_computation.6 | convolution fusion | flops 231211008 | bytes 54398976 | tf_op jit(solution)/shard_map/dot_general | solution.py:115
  277.5 4.8 %copy.55 = bf16[1,256,48,128]{3,2,1,0:T(8,128)(2,1)} copy(bf16[1,256,48,128]{1,3,2,0:T(8,128)(2,1)} %fusion.1) | data formatting | bytes 6291456
  (114 shorter events, 96.4 us)
Async XLA Ops:
  0.6 87.8 %copy-start = (bf16[69,48,128]{2,1,0:T(8,128)(2,1)S(1)}, bf16[69,48,128]{2,1,0:T(8,128)(2,1)}, u32[]{:S(2)}) copy-start(bf16[69,48,128]{2,1,0:T(8,128)(2,1)} %param.10) | copy-start | bytes 2543620
  12.2 12.3 %collective-permute-start = (bf16[1,256,48,1]{1,2,3,0:T(8,128)(2,1)S(1)}, bf16[1,256,48,1]{1,2,3,0:T(8,128)(2,1)S(1)}, u32[]{:S(2)}, u32[]{:S(2)}) collective-permute-start(bf16[1,256,48,1]{1,2,3,0:T(8,128)(2,1)S(1)} %copy.57), channel_id=1, source_target_pairs={{0,1},{1,2},{2,3},{3,0},{4,5},{5,6},{6,7},{7,4},{8,9},{9,10},{10,1... | collective-permute-start | bytes 73736 | tf_op jit(solution)/shard_map/ppermute | solution.py:16
  18.8 8.5 %collective-permute-start.1 = (bf16[1,256,48,1]{1,2,3,0:T(8,128)(2,1)S(1)}, bf16[1,256,48,1]{1,2,3,0:T(8,128)(2,1)S(1)}, u32[]{:S(2)}, u32[]{:S(2)}) collective-permute-start(bf16[1,256,48,1]{1,2,3,0:T(8,128)(2,1)S(1)} %copy.58), channel_id=1, source_target_pairs={{1,0},{2,1},{3,2},{0,3},{5,4},{6,5},{7,6},{4,7},{9,8},{10,9},{11,1... | collective-permute-start | bytes 73736 | tf_op jit(solution)/shard_map/ppermute | solution.py:17
  31.2 17.9 %collective-permute-start.2 = (bf16[1,256,1,130]{3,1,2,0:T(8,128)(2,1)S(1)}, bf16[1,256,1,130]{3,1,2,0:T(8,128)(2,1)S(1)}, u32[]{:S(2)}, u32[]{:S(2)}) collective-permute-start(bf16[1,256,1,130]{3,1,2,0:T(8,128)(2,1)S(1)} %get-tuple-element.121), channel_id=1, source_target_pairs={{0,4},{4,8},{8,12},{1,5},{5,9},{9,13},{2,6},{6,10},{10,14},{3,7},{... | collective-permute-start | bytes 199688 | tf_op jit(solution)/shard_map/ppermute | solution.py:16
  36.1 13.1 %collective-permute-start.3 = (bf16[1,256,1,130]{3,1,2,0:T(8,128)(2,1)S(1)}, bf16[1,256,1,130]{3,1,2,0:T(8,128)(2,1)S(1)}, u32[]{:S(2)}, u32[]{:S(2)}) collective-permute-start(bf16[1,256,1,130]{3,1,2,0:T(8,128)(2,1)S(1)} %get-tuple-element.122), channel_id=1, source_target_pairs={{4,0},{8,4},{12,8},{5,1},{9,5},{13,9},{6,2},{10,6},{14,10},{7,3},{... | collective-permute-start | bytes 199688 | tf_op jit(solution)/shard_map/ppermute | solution.py:17
  38.8 27.7 %all-to-all-start = ((bf16[1,69,16,128]{3,1,0,2:T(8,128)(2,1)}), bf16[1,69,16,128]{3,1,0,2:T(8,128)(2,1)S(1)}, u32[]{:S(2)}, u32[]{:S(2)}) async-start(bf16[1,69,16,128]{3,1,0,2:T(8,128)(2,1)} %broadcast_in_dim.9), calls=%async_computation | async-start | bytes 589824 | tf_op jit(solution)/shard_map/all_to_all | solution.py:91
  49.1 6.6 %copy-start.5 = (bf16[3,3,69,256]{3,2,1,0:T(8,128)(2,1)S(1)}, bf16[3,3,69,256]{3,2,1,0:T(8,128)(2,1)}, u32[]{:S(2)}) copy-start(bf16[3,3,69,256]{3,2,1,0:T(8,128)(2,1)} %param.8) | copy-start | bytes 953860
  63.2 0.7 copy-start.7
  63.9 24.8 %copy-start.8 = (f32[69]{0:T(128)S(1)}, f32[69]{0:T(128)}, u32[]{:S(2)}) copy-start(f32[69]{0:T(128)} %param.11) | copy-start | bytes 832
  66.5 46.9 %all-to-all-start.1 = ((bf16[1,69,48,128]{3,1,0,2:T(8,128)(2,1)}), bf16[1,69,48,128]{3,1,0,2:T(8,128)(2,1)}, u32[]{:S(2)}, u32[]{:S(2)}) async-start(bf16[1,69,48,128]{3,1,0,2:T(8,128)(2,1)} %bitcast.27), calls=%async_computation.1 | async-start | bytes 1769472 | tf_op jit(solution)/shard_map/all_to_all | solution.py:88
  208.8 5.6 %copy-start.2 = (bf16[16,69,3,128]{3,1,2,0:T(8,128)(2,1)}, bf16[16,69,3,128]{3,1,2,0:T(8,128)(2,1)S(1)}, u32[]{:S(2)}) copy-start(bf16[16,69,3,128]{3,1,2,0:T(8,128)(2,1)S(1)} %all_to_all.54) | copy-start | bytes 2543620
  209.6 3.8 %collective-permute-start.4 = (bf16[1,69,48,1]{1,2,3,0:T(8,128)(2,1)S(1)}, bf16[1,69,48,1]{1,2,3,0:T(8,128)(2,1)S(1)}, u32[]{:S(2)}, u32[]{:S(2)}) collective-permute-start(bf16[1,69,48,1]{1,2,3,0:T(8,128)(2,1)S(1)} %copy.50), channel_id=1, source_target_pairs={{0,1},{1,2},{2,3},{3,0},{4,5},{5,6},{6,7},{7,4},{8,9},{9,10},{10,1... | collective-permute-start | bytes 19880 | tf_op jit(solution)/shard_map/ppermute | solution.py:16
  210.1 3.8 %collective-permute-start.5 = (bf16[1,69,48,1]{1,2,3,0:T(8,128)(2,1)S(1)}, bf16[1,69,48,1]{1,2,3,0:T(8,128)(2,1)S(1)}, u32[]{:S(2)}, u32[]{:S(2)}) collective-permute-start(bf16[1,69,48,1]{1,2,3,0:T(8,128)(2,1)S(1)} %copy.51), channel_id=1, source_target_pairs={{1,0},{2,1},{3,2},{0,3},{5,4},{6,5},{7,6},{4,7},{9,8},{10,9},{11,1... | collective-permute-start | bytes 19880 | tf_op jit(solution)/shard_map/ppermute | solution.py:17
  213.9 7.7 %copy-start.3 = (bf16[1,69,48,1]{3,1,2,0:T(8,128)(2,1)}, bf16[1,69,48,1]{3,1,2,0:T(8,128)(2,1)S(1)}, u32[]{:S(2)}) copy-start(bf16[1,69,48,1]{3,1,2,0:T(8,128)(2,1)S(1)} %copy.52) | copy-start | bytes 19876
  214.4 7.2 %copy-start.4 = (bf16[1,69,48,1]{3,1,2,0:T(8,128)(2,1)}, bf16[1,69,48,1]{3,1,2,0:T(8,128)(2,1)S(1)}, u32[]{:S(2)}) copy-start(bf16[1,69,48,1]{3,1,2,0:T(8,128)(2,1)S(1)} %copy.53) | copy-start | bytes 19876
  214.5 7.1 %collective-permute-start.6 = (bf16[1,69,1,130]{3,1,2,0:T(8,128)(2,1)S(1)}, bf16[1,69,1,130]{3,1,2,0:T(8,128)(2,1)S(1)}, u32[]{:S(2)}, u32[]{:S(2)}) collective-permute-start(bf16[1,69,1,130]{3,1,2,0:T(8,128)(2,1)S(1)} %get-tuple-element.125), channel_id=1, source_target_pairs={{0,4},{4,8},{8,12},{1,5},{5,9},{9,13},{2,6},{6,10},{10,14},{3,7},{... | collective-permute-start | bytes 53828 | tf_op jit(solution)/shard_map/ppermute | solution.py:16
  216.5 5.3 %collective-permute-start.7 = (bf16[1,69,1,130]{3,1,2,0:T(8,128)(2,1)S(1)}, bf16[1,69,1,130]{3,1,2,0:T(8,128)(2,1)S(1)}, u32[]{:S(2)}, u32[]{:S(2)}) collective-permute-start(bf16[1,69,1,130]{3,1,2,0:T(8,128)(2,1)S(1)} %get-tuple-element.126), channel_id=1, source_target_pairs={{4,0},{8,4},{12,8},{5,1},{9,5},{13,9},{6,2},{10,6},{14,10},{7,3},{... | collective-permute-start | bytes 53828 | tf_op jit(solution)/shard_map/ppermute | solution.py:17
  219.4 5.1 %copy-start.6 = (bf16[3,3,69,256]{3,2,1,0:T(8,128)(2,1)S(1)}, bf16[3,3,69,256]{3,2,1,0:T(8,128)(2,1)}, u32[]{:S(2)}) copy-start(bf16[3,3,69,256]{3,2,1,0:T(8,128)(2,1)} %param.8) | copy-start | bytes 953860
  258.9 23.4 %copy-start.1 = (bf16[69,48,128]{2,1,0:T(8,128)(2,1)S(1)}, bf16[69,48,128]{2,1,0:T(8,128)(2,1)}, u32[]{:S(2)}) copy-start(bf16[69,48,128]{2,1,0:T(8,128)(2,1)} %param.10) | copy-start | bytes 2543620
where the time goes:
time: 284 us; the launch traced here: 282 us
  matrix products  64.2 us (23%)
  other arithmetic  59.7 us (21%)
  local copies, waits for them, and re-layouts  52.3 us (18%)
  starting transfers between devices  49.9 us (18%)
  blocking collectives  29.9 us (11%)
  waiting for transfers between devices  24.9 us (9%)
    dot_general x9, matrix products, shards(): lax.dot_general(conv_weight[row_tap, col_tap], window, (((0,), (0,)), (()...  53 us
    add x16, other arithmetic, add_member(): return running + smooth(quantity_table - member_values)  46.9 us
    all_to_all x1, blocking collectives, shards(): lax.all_to_all(grad_block, 'member', split_axis=0, concat_axis=2, tiled=T...  29.9 us
    all_to_all x1, waiting for transfers between devices, shards(): lax.all_to_all(predicted_fields, 'member', split_axis=2, concat_axis=0, t...  24.2 us
    unnamed x26, local copies, waits for them, and re-layouts  23.5 us
    all_to_all x1, starting transfers between devices, shards(): lax.all_to_all(predicted_fields, 'member', split_axis=2, concat_axis=0, t...  21.8 us
    dynamic_slice x16, local copies, waits for them, and re-layouts, add_member(): lax.dynamic_index_in_dim(others, member_index, 0, keepdims=True)  13.2 us
    dot_general x9, matrix products, shards(): lax.dot_general(conv_weight[row_tap, col_tap], window, (((1,), (0,)), (()...  10.8 us
  transfers between devices with their start and end apart: 10, of which 3 were waited for; matrix products, arithmetic and copies ran while one was open for 12% of the time, Pallas kernels for 0%

commit v1 on v0

v1 whole, which is shorter than its diff:
```python
import functools

import jax
import jax.numpy as jnp
from jax import lax
from jax.experimental import pallas as pl
from jax.experimental.pallas import tpu as pltpu
from jax.sharding import PartitionSpec as P

SMOOTHING2 = 0.0625
MESH = pl.DeviceIdType.MESH
BF = jnp.bfloat16
F32 = jnp.float32
OP = 72
LANES = 128


def smooth(d):
    return d * lax.rsqrt(d * d + SMOOTHING2)


def lanes_of(shape):
    return lax.broadcasted_iota(jnp.int32, shape, len(shape) - 1)


def exchange_kernel(
    members, lats, lons, rounds, channels,
    xt, wf, off, obs, wv,
    pred, grad, halo_l, halo_r,
    xs, acc, edge, edge_l, edge_r, block, vals, gout, cols, cols_bf,
    xsem, hsend, hrecv, esend, erecv, psend, precv, gsend, grecv, rsend, rrecv, csend, crecv,
):
    me = lax.axis_index("member")
    lat = lax.axis_index("lat")
    lon = lax.axis_index("lon")
    left = lax.rem(lon + lons - 1, lons)
    right = lax.rem(lon + 1, lons)
    rows = rounds * members
    has_up = lat > 0
    has_down = lat < lats - 1

    def chunk_copy(s):
        part = pl.ds(members * s, members)
        return pltpu.make_async_copy(xt.at[part], xs.at[pl.ds(1 + members * s, members)], xsem.at[s])

    for s in (1, 0, 2):
        chunk_copy(s).start()

    barrier = pltpu.get_barrier_semaphore()

    def greet(d, carry):
        pl.semaphore_signal(
            barrier, inc=1, device_id=(lax.rem(me + d, members), lat, lon), device_id_type=MESH
        )
        return carry

    lax.fori_loop(1, members, greet, 0)
    for side in (left, right):
        pl.semaphore_signal(barrier, inc=1, device_id=(me, lat, side), device_id_type=MESH)

    @pl.when(has_up)
    def _():
        pl.semaphore_signal(barrier, inc=1, device_id=(me, lat - 1, lon), device_id_type=MESH)

    @pl.when(has_down)
    def _():
        pl.semaphore_signal(barrier, inc=1, device_id=(me, lat + 1, lon), device_id_type=MESH)

    pl.semaphore_wait(barrier, members - 1 + 2 + has_up.astype(jnp.int32) + has_down.astype(jnp.int32))

    def row_up():
        return pltpu.make_async_remote_copy(
            xt.at[0], xs.at[rows + 1], hsend.at[0], hrecv.at[0],
            device_id=(me, lat - 1, lon), device_id_type=MESH)

    def row_down():
        return pltpu.make_async_remote_copy(
            xt.at[rows - 1], xs.at[0], hsend.at[1], hrecv.at[1],
            device_id=(me, lat + 1, lon), device_id_type=MESH)

    def grow_up():
        return pltpu.make_async_remote_copy(
            grad.at[1], grad.at[rows + 1], rsend.at[0], rrecv.at[0],
            device_id=(me, lat - 1, lon), device_id_type=MESH)

    def grow_down():
        return pltpu.make_async_remote_copy(
            grad.at[rows], grad.at[0], rsend.at[1], rrecv.at[1],
            device_id=(me, lat + 1, lon), device_id_type=MESH)

    @pl.when(has_up)
    def _():
        row_up().start()

    @pl.when(has_down)
    def _():
        row_down().start()

    @pl.when(jnp.logical_not(has_up))
    def _():
        xs[0] = jnp.zeros_like(xs[0])
        grad[0] = jnp.zeros_like(grad[0])

    @pl.when(jnp.logical_not(has_down))
    def _():
        xs[rows + 1] = jnp.zeros_like(xs[rows + 1])
        grad[rows + 1] = jnp.zeros_like(grad[rows + 1])

    lane = lanes_of((OP, LANES))

    def edge_copy(s, side, dst, k):
        return pltpu.make_async_remote_copy(
            edge.at[s], dst.at[s], esend.at[s, k], erecv.at[s, k],
            device_id=(me, lat, side), device_id_type=MESH)

    def convolve(s):
        collected = jnp.zeros((OP, LANES), F32)
        for q in range(members // 2):
            r = members * s + 2 * q
            taps = jnp.concatenate(
                [xs[r:r + 3].reshape(3 * channels, LANES), xs[r + 1:r + 4].reshape(3 * channels, LANES)],
                axis=1)
            res = jnp.dot(wf[...], taps, preferred_element_type=F32)
            for h in range(2):
                i = 2 * q + h
                part = res[:, h * LANES:(h + 1) * LANES]
                a0, a1, a2 = part[:OP], part[OP:2 * OP], part[2 * OP:]
                acc[members * s + i] = (
                    a1
                    + jnp.where(lane == 0, 0.0, pltpu.roll(a0, 1, 1))
                    + jnp.where(lane == LANES - 1, 0.0, pltpu.roll(a2, LANES - 1, 1)))
                collected = jnp.where(lane == i, pltpu.roll(a0, 1 + i, 1), collected)
                mine = a2 if i + 64 == 0 else pltpu.roll(a2, 64 + i, 1)
                collected = jnp.where(lane == 64 + i, mine, collected)
        edge[s] = collected
        edge_copy(s, right, edge_l, 0).start()
        edge_copy(s, left, edge_r, 1).start()

    def pred_copy(s, d, to):
        other = lax.rem(me + d, members) if to else lax.rem(me + members - d, members)
        slot = me if to else other
        return pltpu.make_async_remote_copy(
            pred.at[members * s + other], block.at[s, slot], psend.at[s, d], precv.at[s, slot],
            device_id=(other, lat, lon), device_id_type=MESH)

    def finish(s):
        edge_copy(s, right, edge_l, 0).wait_recv()
        edge_copy(s, left, edge_r, 1).wait_recv()
        for i in range(members):
            from_left = edge_l[s] if i == 0 else pltpu.roll(edge_l[s], LANES - i, 1)
            from_right = pltpu.roll(edge_r[s], 63 - i, 1)
            total = acc[members * s + i] + off[...]
            total = total + jnp.where(lane == 0, from_left, 0.0)
            total = total + jnp.where(lane == LANES - 1, from_right, 0.0)
            pred[members * s + i] = total.astype(BF)

        def send(d, carry):
            pred_copy(s, d, True).start()
            return carry

        lax.fori_loop(1, members, send, 0)
        block[s, me] = pred[members * s + me]

    for s in (1, 0, 2):
        if s == 1:
            for k in range(rounds):
                chunk_copy(k).wait()
        if s == 0:
            @pl.when(has_up)
            def _():
                row_down().wait_recv()
        if s == 2:
            @pl.when(has_down)
            def _():
                row_up().wait_recv()
        convolve(s)
        if s == 0:
            finish(1)
        if s == 2:
            finish(0)
            finish(2)

    def grad_copy(s, d, to):
        other = lax.rem(me + d, members) if to else lax.rem(me + members - d, members)
        owner = me if to else other
        return pltpu.make_async_remote_copy(
            gout.at[s, other], grad.at[1 + members * s + owner], gsend.at[s, d], grecv.at[s, owner],
            device_id=(other, lat, lon), device_id_type=MESH)

    for s in (0, 2, 1):
        def arrive(d, carry):
            pred_copy(s, d, False).wait_recv()
            return carry

        lax.fori_loop(1, members, arrive, 0)
        vals[...] = block[s].astype(F32)

        def slab(k, carry):
            part = pl.ds(pl.multiple_of(8 * k, 8), 8)
            v = vals[:, part, :]
            total = jnp.zeros_like(v)
            for step in range(1, members // 2):
                t = smooth(v - jnp.concatenate([v[step:], v[:step]], axis=0))
                total = total + t - jnp.concatenate([t[members - step:], t[:members - step]], axis=0)
            t = smooth(v[:members // 2] - v[members // 2:])
            total = total + jnp.concatenate([t, -t], axis=0)
            seen = obs[s, part, :].astype(F32)
            vals[:, part, :] = wv[s, part, :] * (smooth(v - seen) - total / (members - 1))
            return carry

        lax.fori_loop(0, OP // 8, slab, 0)
        gout[s] = vals[...].astype(BF)

        def send(d, carry):
            grad_copy(s, d, True).start()
            return carry

        lax.fori_loop(1, members, send, 0)
        grad[1 + members * s + me] = gout[s, me]

    def collect(g):
        row = grad[g].astype(F32)
        now = jnp.where(lane == g, pltpu.roll(row, g, 1), cols[...])
        cols[...] = jnp.where(lane == 64 + g, pltpu.roll(row, 65 + g, 1), now)

    cols[...] = jnp.zeros_like(cols)
    for s in (0, 2, 1):
        def arrive_back(d, carry):
            grad_copy(s, d, False).wait_recv()
            return carry

        lax.fori_loop(1, members, arrive_back, 0)
        if s == 0:
            @pl.when(has_up)
            def _():
                grow_up().start()
        if s == 2:
            @pl.when(has_down)
            def _():
                grow_down().start()

        def gather(i, carry):
            collect(1 + members * s + i)
            return carry

        lax.fori_loop(0, members, gather, 0)

    @pl.when(has_up)
    def _():
        grow_down().wait_recv()

    @pl.when(has_down)
    def _():
        grow_up().wait_recv()

    collect(0)
    collect(rows + 1)
    cols_bf[...] = cols[...].astype(BF)

    def col_copy(side, dst, k):
        return pltpu.make_async_remote_copy(
            cols_bf, dst, csend.at[k], crecv.at[k], device_id=(me, lat, side), device_id_type=MESH)

    col_copy(right, halo_l, 0).start()
    col_copy(left, halo_r, 1).start()

    for s in range(rounds):
        edge_copy(s, right, edge_l, 0).wait_send()
        edge_copy(s, left, edge_r, 1).wait_send()

        def left_device(d, carry):
            pred_copy(s, d, True).wait_send()
            grad_copy(s, d, True).wait_send()
            return carry

        lax.fori_loop(1, members, left_device, 0)

    @pl.when(has_up)
    def _():
        row_up().wait_send()
        grow_up().wait_send()

    @pl.when(has_down)
    def _():
        row_down().wait_send()
        grow_down().wait_send()

    col_copy(right, halo_l, 0).wait()
    col_copy(left, halo_r, 1).wait()


def backward_kernel(block_rows, depth, channels, grad, halo_l, halo_r, wb, out, gs, flat):
    step = pl.program_id(0)
    lane = lanes_of((OP, LANES))
    first = step * block_rows
    hl = halo_l[...].astype(F32)
    hr = halo_r[...].astype(F32)

    def widen(i, carry):
        g = first + i
        row = grad[g].astype(F32)
        after = jnp.where(lane == LANES - 1, pltpu.roll(hr, LANES - 1 - g, 1), pltpu.roll(row, LANES - 1, 1))
        before = jnp.where(lane == 0, pltpu.roll(hl, lax.rem(LANES + 64 - g, LANES), 1), pltpu.roll(row, 1, 1))
        full = jnp.concatenate([after, row, before, jnp.zeros((depth - 3 * OP, LANES), F32)], axis=0)
        gs[i] = full.astype(BF)
        return carry

    lax.fori_loop(0, block_rows + 2, widen, 0)
    for q in range(block_rows // 2):
        r = 2 * q
        taps = jnp.concatenate(
            [gs[r:r + 3].reshape(3 * depth, LANES), gs[r + 1:r + 4].reshape(3 * depth, LANES)], axis=1)
        res = jnp.dot(wb[...], taps, preferred_element_type=F32)
        for h in range(2):
            flat[pl.ds(r + h, channels, stride=block_rows), :] = res[:, h * LANES:(h + 1) * LANES]
    out[...] = flat[...].reshape(channels, block_rows, LANES).astype(BF)


def shards(members, lats, lons, layer_inputs, conv_weight, channel_offset, observed, var_weight):
    channels, rows, cols = layer_inputs.shape[1:]
    outputs = conv_weight.shape[2]
    rounds = rows // members
    total_rows = rows * lats
    depth = 224
    me = lax.axis_index("member")
    lat = lax.axis_index("lat")

    xt = layer_inputs[0].transpose(1, 0, 2)
    weight = jnp.pad(conv_weight, ((0, 0), (0, 0), (0, OP - outputs), (0, 0)))
    wf = weight.transpose(1, 2, 0, 3).reshape(3 * OP, 3 * channels)
    wb = jnp.pad(weight[::-1].reshape(3, 3 * OP, channels), ((0, 0), (0, depth - 3 * OP), (0, 0)))
    wb = wb.reshape(3 * depth, channels).T
    off = jnp.broadcast_to(jnp.pad(channel_offset, (0, OP - outputs))[:, None], (OP, LANES))
    mine = lax.dynamic_index_in_dim(observed.reshape(outputs, rounds, members, cols), me, 2, keepdims=False)
    obs = jnp.pad(mine.transpose(1, 0, 2), ((0, 0), (0, OP - outputs), (0, 0)))
    row_index = (lat * rows + members * jnp.arange(rounds) + me).astype(F32)
    lat_weight = jnp.cos((-80.0 + 160.0 * (row_index + 0.5) / float(total_rows)) * (jnp.pi / 180.0))
    wv = lat_weight[:, None] * jnp.pad(var_weight, (0, OP - outputs))[None, :]
    wv = jnp.broadcast_to(wv[:, :, None], (rounds, OP, LANES))

    vmem = pl.BlockSpec(memory_space=pltpu.VMEM)
    dma = pltpu.SemaphoreType.DMA
    pred, grad, halo_l, halo_r = pl.pallas_call(
        functools.partial(exchange_kernel, members, lats, lons, rounds, channels),
        out_shape=(
            jax.ShapeDtypeStruct((rows, OP, LANES), BF),
            jax.ShapeDtypeStruct((rows + 2, OP, LANES), BF),
            jax.ShapeDtypeStruct((OP, LANES), BF),
            jax.ShapeDtypeStruct((OP, LANES), BF),
        ),
        in_specs=[pl.BlockSpec(memory_space=pl.ANY)] + [vmem] * 4,
        out_specs=(vmem,) * 4,
        scratch_shapes=[
            pltpu.VMEM((rows + 2, channels, LANES), BF),
            pltpu.VMEM((rows, OP, LANES), F32),
            pltpu.VMEM((rounds, OP, LANES), F32),
            pltpu.VMEM((rounds, OP, LANES), F32),
            pltpu.VMEM((rounds, OP, LANES), F32),
            pltpu.VMEM((rounds, members, OP, LANES), BF),
            pltpu.VMEM((members, OP, LANES), F32),
            pltpu.VMEM((rounds, members, OP, LANES), BF),
            pltpu.VMEM((OP, LANES), F32),
            pltpu.VMEM((OP, LANES), BF),
            dma((rounds,)), dma((2,)), dma((2,)), dma((rounds, 2)), dma((rounds, 2)),
            dma((rounds, members)), dma((rounds, members)), dma((rounds, members)), dma((rounds, members)),
            dma((2,)), dma((2,)), dma((2,)), dma((2,)),
        ],
        compiler_params=pltpu.CompilerParams(
            collective_id=0, has_side_effects=True, vmem_limit_bytes=56 * 2**20),
        name="exchange",
    )(xt, wf, off, obs, wv)

    block_rows = 16
    slope = pl.pallas_call(
        functools.partial(backward_kernel, block_rows, depth, channels),
        grid=(rows // block_rows,),
        out_shape=jax.ShapeDtypeStruct((channels, rows, LANES), BF),
        in_specs=[vmem] * 4,
        out_specs=pl.BlockSpec((channels, block_rows, LANES), lambda i: (0, i, 0)),
        scratch_shapes=[
            pltpu.VMEM((block_rows + 2, depth, LANES), BF),
            pltpu.VMEM((channels * block_rows, LANES), F32),
        ],
        compiler_params=pltpu.CompilerParams(vmem_limit_bytes=56 * 2**20),
        name="backward",
    )(grad, halo_l, halo_r, wb)
    return pred[:, :outputs].transpose(1, 0, 2)[None], slope[None]


def solution(mesh):
    members, lats, lons = (mesh.shape[a] for a in ("member", "lat", "lon"))
    in_specs = (P("member", None, "lat", "lon"), P(), P(), P(None, "lat", "lon"), P())
    out_specs = (P("member", None, "lat", "lon"), P("member", None, "lat", "lon"))
    return jax.shard_map(
        functools.partial(shards, members, lats, lons),
        mesh=mesh, in_specs=in_specs, out_specs=out_specs, check_vma=False)
```

time: 284 us -> 88.9 us (0.31)
  the two profiles are of different devices: /device:TPU:1 before, /device:TPU:2 now
where the time goes in v1:
time: 88.9 us; the launch traced here: 88.6 us
  Pallas kernels  75.4 us (85%)
  local copies, waits for them, and re-layouts  12.4 us (14%)
    pallas_call x1, Pallas kernels, shards(): pl.pallas_call(functools.partial(exchange_kernel, members, lats, lons, ro...  64.2 us
    pallas_call x1, Pallas kernels, shards(): pl.pallas_call(functools.partial(backward_kernel, block_rows, depth, chan...  11.2 us
    unnamed x10, local copies, waits for them, and re-layouts  7.34 us

profile of v1, /device:TPU:2, one launch (start us, length us, event | category | flops | bytes accessed | tf_op | source)
XLA Modules:
  0.0 88.6 jit_solution(8399503210861710016)
XLA Ops:
  0.6 0.0 copy-start
  0.7 1.1 %copy-done = bf16[69,48,128]{2,1,0:T(8,128)(2,1)S(1)} copy-done((bf16[69,48,128]{2,1,0:T(8,128)(2,1)S(1)}, bf16[69,48,128]{2,1,0:T(8,128)(2,1)}, u32[]{:S(2)}) %copy-start) | copy-done | bytes 847896
  1.8 0.1 constant_dynamic-slice_fusion
  1.9 0.6 pad.21.obs
  2.6 0.7 pad.22
  3.3 0.1 broadcast_multiply_fusion
  3.4 0.7 broadcast_in_dim.9.wv
  4.1 1.0 %fusion = (bf16[3,3,72,256]{3,2,1,0:T(8,128)(2,1)S(1)}, bf16[3,72,3,256]{3,1,0,2:T(8,128)(2,1)S(1)}) fusion(bf16[3,3,69,256]{3,2,1,0:T(8,128)(2,1)} %param.6), kind=kLoop, calls=%fused_computation.7 | loop fusion | bytes 981504 | tf_op jit(solution)/shard_map/jit(_pad)/pad | solution.py:329
  5.1 0.2 copy.13
  5.3 0.8 copy.18
  6.1 0.0 copy-start.2
  6.1 4.4 %copy.21 = bf16[1,256,48,128]{3,1,2,0:T(8,128)(2,1)} copy(bf16[1,256,48,128]{3,2,1,0:T(8,128)(2,1)} %param.5) | data formatting | bytes 6291456 | tf_op args[0]
  10.5 0.0 copy-done.2
  10.5 0.7 broadcast_in_dim.8.off
  11.2 64.2 %exchange.1 = (bf16[48,72,128]{2,1,0:T(8,128)(2,1)}, bf16[50,72,128]{2,1,0:T(8,128)(2,1)}, bf16[72,128]{1,0:T(8,128)(2,1)}, bf16[72,128]{1,0:T(8,128)(2,1)}) custom-call(bf16[48,256,128]{2,1,0:T(8,128)(2,1)} %bitcast.25, bf16[216,768]{1,0:T(8,128)(2,1)} %bitcast.30, f32[72,128]{1,0:T(8,128)} %broadcast_in_dim.8.off, bf16[3,72,128]{2,1,0:T(8,128)(2,1)} %pad.21.obs, ...), custom_call_target="tpu_custom_call" | custom-call | tf_op jit(solution)/shard_map/exchange/pallas_call | solution.py:343
  75.4 0.0 copy-start.1
  75.5 0.9 %copy.15 = bf16[672,256]{0,1:T(8,128)(2,1)} copy(bf16[672,256]{1,0:T(8,128)(2,1)S(1)} %bitcast.29) | data formatting | bytes 688128 | tf_op jit(solution)/shard_map/reshape | solution.py:332
  76.4 11.2 %backward.1 = bf16[256,48,128]{2,1,0:T(8,128)(2,1)} custom-call(bf16[50,72,128]{2,1,0:T(8,128)(2,1)} %get-tuple-element.7.grad, bf16[72,128]{1,0:T(8,128)(2,1)} %get-tuple-element.8.halo_l, bf16[72,128]{1,0:T(8,128)(2,1)} %get-tuple-element.9.halo_r, bf16[256,672]{1,0:T(8,128)(2,1)} %bitcast.28), custom_call_target="tpu_custom_call" | custom-call | tf_op jit(solution)/shard_map/backward/pallas_call | solution.py:374
  87.6 0.0 copy-done.1
  87.6 0.1 slice_bitcast_fusion
  87.6 1.0 %copy.16 = bf16[1,69,48,128]{3,2,1,0:T(8,128)(2,1)} copy(bf16[1,69,48,128]{3,1,2,0:T(8,128)(2,1)S(1)} %slice_bitcast_fusion) | data formatting | bytes 1695744
  (5 shorter events, 0.1 us)
Async XLA Ops:
  0.6 1.2 %copy-start = (bf16[69,48,128]{2,1,0:T(8,128)(2,1)S(1)}, bf16[69,48,128]{2,1,0:T(8,128)(2,1)}, u32[]{:S(2)}) copy-start(bf16[69,48,128]{2,1,0:T(8,128)(2,1)} %param.8) | copy-start | bytes 2543620
  6.1 4.4 %copy-start.2 = (f32[69]{0:T(128)S(1)}, f32[69]{0:T(128)}, u32[]{:S(2)}) copy-start(f32[69]{0:T(128)} %param.7) | copy-start | bytes 832
  75.4 12.2 %copy-start.1 = (bf16[48,72,128]{2,1,0:T(8,128)(2,1)S(1)}, bf16[48,72,128]{2,1,0:T(8,128)(2,1)}, u32[]{:S(2)}) copy-start(bf16[48,72,128]{2,1,0:T(8,128)(2,1)} %get-tuple-element.6) | copy-start | bytes 2654212

commit v2 on v1

--- a/solution.py
+++ b/solution.py
@@ -1,4 +1,5 @@
 import functools
+import math
 
 import jax
 import jax.numpy as jnp
@@ -23,12 +24,18 @@
     return lax.broadcasted_iota(jnp.int32, shape, len(shape) - 1)
 
 
+def column(vector, count):
+    rows = lax.broadcasted_iota(jnp.int32, (OP, count), 0)
+    spread = jnp.where(rows == lanes_of((OP, count)), jnp.broadcast_to(vector, (OP, count)), 0.0)
+    return jnp.broadcast_to(jnp.sum(spread, axis=1, keepdims=True), (OP, LANES))
+
+
 def exchange_kernel(
-    members, lats, lons, rounds, channels,
-    xt, wf, off, obs, wv,
-    pred, grad, halo_l, halo_r,
-    xs, acc, edge, edge_l, edge_r, block, vals, gout, cols, cols_bf,
-    xsem, hsend, hrecv, esend, erecv, psend, precv, gsend, grecv, rsend, rrecv, csend, crecv,
+    members, lats, lons, rounds, channels, outputs,
+    xn, weight, observed, offset_in, var_in,
+    pred, grad, halo_l, halo_r, wb,
+    xv, xs, stage, wv, wf, obn, obs, offset, var, off, varb, acc, edge, edge_l, edge_r, block, vals, gout, cols, cols_bf,
+    xsem, wsem, osem, smem, hsend, hrecv, esend, erecv, psend, precv, gsend, grecv, rsend, rrecv, csend, crecv,
 ):
     me = lax.axis_index("member")
     lat = lax.axis_index("lat")
@@ -38,13 +45,30 @@
     rows = rounds * members
     has_up = lat > 0
     has_down = lat < lats - 1
-
-    def chunk_copy(s):
-        part = pl.ds(members * s, members)
-        return pltpu.make_async_copy(xt.at[part], xs.at[pl.ds(1 + members * s, members)], xsem.at[s])
-
-    for s in (1, 0, 2):
-        chunk_copy(s).start()
+    blocks = (2, 3, 1, 4, 0, 5)
+
+    def block_copy(j):
+        return pltpu.make_async_copy(xn.at[:, pl.ds(8 * j, 8), :], xv.at[j], xsem.at[j])
+
+    def weight_copy():
+        return pltpu.make_async_copy(weight, wv, wsem)
+
+    def observed_copy(s):
+        start = pl.multiple_of(members * s + 8 * (me // 8), 8)
+        return pltpu.make_async_copy(observed.at[:, pl.ds(start, 8), :], obn.at[s], osem.at[s])
+
+    def small_copy(k):
+        return pltpu.make_async_copy((offset_in, var_in)[k], (offset, var)[k], smem.at[k])
+
+    for j in blocks[:2]:
+        block_copy(j).start()
+    weight_copy().start()
+    small_copy(0).start()
+    small_copy(1).start()
+    for j in blocks[2:]:
+        block_copy(j).start()
+    for s in range(rounds):
+        observed_copy(s).start()
 
     barrier = pltpu.get_barrier_semaphore()
 
@@ -66,16 +90,14 @@
     def _():
         pl.semaphore_signal(barrier, inc=1, device_id=(me, lat + 1, lon), device_id_type=MESH)
 
-    pl.semaphore_wait(barrier, members - 1 + 2 + has_up.astype(jnp.int32) + has_down.astype(jnp.int32))
-
     def row_up():
         return pltpu.make_async_remote_copy(
-            xt.at[0], xs.at[rows + 1], hsend.at[0], hrecv.at[0],
+            xs.at[1], xs.at[rows + 1], hsend.at[0], hrecv.at[0],
             device_id=(me, lat - 1, lon), device_id_type=MESH)
 
     def row_down():
         return pltpu.make_async_remote_copy(
-            xt.at[rows - 1], xs.at[0], hsend.at[1], hrecv.at[1],
+            xs.at[rows], xs.at[0], hsend.at[1], hrecv.at[1],
             device_id=(me, lat + 1, lon), device_id_type=MESH)
 
     def grow_up():
@@ -87,14 +109,6 @@
         return pltpu.make_async_remote_copy(
             grad.at[rows], grad.at[0], rsend.at[1], rrecv.at[1],
             device_id=(me, lat + 1, lon), device_id_type=MESH)
-
-    @pl.when(has_up)
-    def _():
-        row_up().start()
-
-    @pl.when(has_down)
-    def _():
-        row_down().start()
 
     @pl.when(jnp.logical_not(has_up))
     def _():
@@ -161,24 +175,65 @@
         lax.fori_loop(1, members, send, 0)
         block[s, me] = pred[members * s + me]
 
-    for s in (1, 0, 2):
-        if s == 1:
-            for k in range(rounds):
-                chunk_copy(k).wait()
-        if s == 0:
-            @pl.when(has_up)
-            def _():
-                row_down().wait_recv()
-        if s == 2:
-            @pl.when(has_down)
-            def _():
-                row_up().wait_recv()
-        convolve(s)
-        if s == 0:
-            finish(1)
-        if s == 2:
-            finish(0)
-            finish(2)
+    def relay(j):
+        block_copy(j).wait()
+        buf = stage.at[j % 2]
+        buf[...] = xv[j].astype(F32).reshape(8 * channels, LANES)
+        for r in range(8):
+            xs[1 + 8 * j + r] = buf[pl.ds(r, channels, stride=8), :].astype(BF)
+
+    weight_copy().wait()
+    for a in range(3):
+        for b in range(3):
+            full = jnp.concatenate(
+                [wv[a, b].astype(F32), jnp.zeros((OP - outputs, channels), F32)], axis=0)
+            wf[b * OP:(b + 1) * OP, a * channels:(a + 1) * channels] = full.astype(BF)
+    small_copy(0).wait()
+    off[...] = column(offset[...], outputs)
+    for j in blocks[:4]:
+        relay(j)
+    pl.semaphore_wait(barrier, members - 1 + 2 + has_up.astype(jnp.int32) + has_down.astype(jnp.int32))
+    convolve(1)
+    relay(0)
+    relay(5)
+    @pl.when(has_up)
+    def _():
+        row_up().start()
+
+    @pl.when(has_down)
+    def _():
+        row_down().start()
+    for t in range(3):
+        taps = [wv[2 - t, b].astype(F32) for b in range(3)]
+        pad = jnp.zeros((OP - outputs, channels), F32)
+        tall = jnp.concatenate(
+            [taps[0], pad, taps[1], pad, taps[2], pad, jnp.zeros((channels - 3 * OP, channels), F32)], axis=0)
+        wb[:, t * channels:(t + 1) * channels] = tall.T.astype(BF)
+    finish(1)
+
+    @pl.when(has_up)
+    def _():
+        row_down().wait_recv()
+
+    convolve(0)
+
+    @pl.when(has_down)
+    def _():
+        row_up().wait_recv()
+
+    convolve(2)
+    finish(0)
+    finish(2)
+
+    small_copy(1).wait()
+    varb[...] = column(var[...], outputs)
+    variable = lax.broadcasted_iota(jnp.int32, (OP, LANES), 0)
+    for s in range(rounds):
+        observed_copy(s).wait()
+        buf = stage.at[s % 2]
+        buf[0:8 * outputs, :] = obn[s].astype(F32).reshape(8 * outputs, LANES)
+        picked = buf[pl.ds(lax.rem(me, 8), OP, stride=8), :]
+        obs[s] = jnp.where(variable < outputs, picked, 0.0)
 
     def grad_copy(s, d, to):
         other = lax.rem(me + d, members) if to else lax.rem(me + members - d, members)
@@ -194,6 +249,9 @@
 
         lax.fori_loop(1, members, arrive, 0)
         vals[...] = block[s].astype(F32)
+        row_index = jnp.full((8, LANES), lat * rows + members * s + me, jnp.int32).astype(F32)
+        angle = -80.0 + 160.0 * (row_index + 0.5) / float(rows * lats)
+        lat_weight = jnp.cos(angle * (math.pi / 180.0))
 
         def slab(k, carry):
             part = pl.ds(pl.multiple_of(8 * k, 8), 8)
@@ -204,8 +262,8 @@
                 total = total + t - jnp.concatenate([t[members - step:], t[:members - step]], axis=0)
             t = smooth(v[:members // 2] - v[members // 2:])
             total = total + jnp.concatenate([t, -t], axis=0)
-            seen = obs[s, part, :].astype(F32)
-            vals[:, part, :] = wv[s, part, :] * (smooth(v - seen) - total / (members - 1))
+            scale = lat_weight * varb[part, :]
+            vals[:, part, :] = scale * (smooth(v - obs[s, part, :]) - total / (members - 1))
             return carry
 
         lax.fori_loop(0, OP // 8, slab, 0)
@@ -289,69 +347,66 @@
     col_copy(left, halo_r, 1).wait()
 
 
-def backward_kernel(block_rows, depth, channels, grad, halo_l, halo_r, wb, out, gs, flat):
+def backward_kernel(
+    block_rows, pitch, channels, outputs, grad, halo_l, halo_r, wb, rows_in, pred, slope, gs, flat, flat_p
+):
     step = pl.program_id(0)
     lane = lanes_of((OP, LANES))
     first = step * block_rows
     hl = halo_l[...].astype(F32)
     hr = halo_r[...].astype(F32)
-
-    def widen(i, carry):
+    for i in range(block_rows + 2):
         g = first + i
         row = grad[g].astype(F32)
         after = jnp.where(lane == LANES - 1, pltpu.roll(hr, LANES - 1 - g, 1), pltpu.roll(row, LANES - 1, 1))
         before = jnp.where(lane == 0, pltpu.roll(hl, lax.rem(LANES + 64 - g, LANES), 1), pltpu.roll(row, 1, 1))
-        full = jnp.concatenate([after, row, before, jnp.zeros((depth - 3 * OP, LANES), F32)], axis=0)
+        full = jnp.concatenate([after, row, before, jnp.zeros((channels - 3 * OP, LANES), F32)], axis=0)
         gs[i] = full.astype(BF)
-        return carry
-
-    lax.fori_loop(0, block_rows + 2, widen, 0)
+    for i in range(block_rows):
+        flat_p[pl.ds(i, OP, stride=pitch), :] = rows_in[first + i].astype(F32)
+    pred[...] = flat_p[...].reshape(OP, pitch, LANES)[:outputs, :block_rows].astype(BF)
     for q in range(block_rows // 2):
         r = 2 * q
         taps = jnp.concatenate(
-            [gs[r:r + 3].reshape(3 * depth, LANES), gs[r + 1:r + 4].reshape(3 * depth, LANES)], axis=1)
+            [gs[r:r + 3].reshape(3 * channels, LANES), gs[r + 1:r + 4].reshape(3 * channels, LANES)], axis=1)
         res = jnp.dot(wb[...], taps, preferred_element_type=F32)
         for h in range(2):
-            flat[pl.ds(r + h, channels, stride=block_rows), :] = res[:, h * LANES:(h + 1) * LANES]
-    out[...] = flat[...].reshape(channels, block_rows, LANES).astype(BF)
+            flat[pl.ds(r + h, channels, stride=pitch), :] = res[:, h * LANES:(h + 1) * LANES]
+    slope[...] = flat[...].reshape(channels, pitch, LANES)[:, :block_rows].astype(BF)
 
 
 def shards(members, lats, lons, layer_inputs, conv_weight, channel_offset, observed, var_weight):
-    channels, rows, cols = layer_inputs.shape[1:]
+    channels, rows = layer_inputs.shape[1:3]
     outputs = conv_weight.shape[2]
     rounds = rows // members
-    total_rows = rows * lats
-    depth = 224
-    me = lax.axis_index("member")
-    lat = lax.axis_index("lat")
-
-    xt = layer_inputs[0].transpose(1, 0, 2)
-    weight = jnp.pad(conv_weight, ((0, 0), (0, 0), (0, OP - outputs), (0, 0)))
-    wf = weight.transpose(1, 2, 0, 3).reshape(3 * OP, 3 * channels)
-    wb = jnp.pad(weight[::-1].reshape(3, 3 * OP, channels), ((0, 0), (0, depth - 3 * OP), (0, 0)))
-    wb = wb.reshape(3 * depth, channels).T
-    off = jnp.broadcast_to(jnp.pad(channel_offset, (0, OP - outputs))[:, None], (OP, LANES))
-    mine = lax.dynamic_index_in_dim(observed.reshape(outputs, rounds, members, cols), me, 2, keepdims=False)
-    obs = jnp.pad(mine.transpose(1, 0, 2), ((0, 0), (0, OP - outputs), (0, 0)))
-    row_index = (lat * rows + members * jnp.arange(rounds) + me).astype(F32)
-    lat_weight = jnp.cos((-80.0 + 160.0 * (row_index + 0.5) / float(total_rows)) * (jnp.pi / 180.0))
-    wv = lat_weight[:, None] * jnp.pad(var_weight, (0, OP - outputs))[None, :]
-    wv = jnp.broadcast_to(wv[:, :, None], (rounds, OP, LANES))
 
     vmem = pl.BlockSpec(memory_space=pltpu.VMEM)
+    hbm = pl.BlockSpec(memory_space=pltpu.HBM)
     dma = pltpu.SemaphoreType.DMA
-    pred, grad, halo_l, halo_r = pl.pallas_call(
-        functools.partial(exchange_kernel, members, lats, lons, rounds, channels),
+    per_member = dma((rounds, members))
+    pred_rows, grad, halo_l, halo_r, wb = pl.pallas_call(
+        functools.partial(exchange_kernel, members, lats, lons, rounds, channels, outputs),
         out_shape=(
             jax.ShapeDtypeStruct((rows, OP, LANES), BF),
             jax.ShapeDtypeStruct((rows + 2, OP, LANES), BF),
             jax.ShapeDtypeStruct((OP, LANES), BF),
             jax.ShapeDtypeStruct((OP, LANES), BF),
+            jax.ShapeDtypeStruct((channels, 3 * channels), BF),
         ),
-        in_specs=[pl.BlockSpec(memory_space=pl.ANY)] + [vmem] * 4,
-        out_specs=(vmem,) * 4,
+        in_specs=[hbm] * 5,
+        out_specs=(vmem,) * 5,
         scratch_shapes=[
+            pltpu.VMEM((rows // 8, channels, 8, LANES), BF),
             pltpu.VMEM((rows + 2, channels, LANES), BF),
+            pltpu.VMEM((2, 8 * channels, LANES), F32),
+            pltpu.VMEM((3, 3, outputs, channels), BF),
+            pltpu.VMEM((3 * OP, 3 * channels), BF),
+            pltpu.VMEM((rounds, outputs, 8, LANES), BF),
+            pltpu.VMEM((rounds, OP, LANES), F32),
+            pltpu.VMEM((1, outputs), F32),
+            pltpu.VMEM((1, outputs), F32),
+            pltpu.VMEM((OP, LANES), F32),
+            pltpu.VMEM((OP, LANES), F32),
             pltpu.VMEM((rows, OP, LANES), F32),
             pltpu.VMEM((rounds, OP, LANES), F32),
             pltpu.VMEM((rounds, OP, LANES), F32),
@@ -361,30 +416,38 @@
             pltpu.VMEM((rounds, members, OP, LANES), BF),
             pltpu.VMEM((OP, LANES), F32),
             pltpu.VMEM((OP, LANES), BF),
-            dma((rounds,)), dma((2,)), dma((2,)), dma((rounds, 2)), dma((rounds, 2)),
-            dma((rounds, members)), dma((rounds, members)), dma((rounds, members)), dma((rounds, members)),
+            dma((rows // 8,)), dma, dma((rounds,)), dma((2,)),
+            dma((2,)), dma((2,)), dma((rounds, 2)), dma((rounds, 2)),
+            per_member, per_member, per_member, per_member,
             dma((2,)), dma((2,)), dma((2,)), dma((2,)),
         ],
         compiler_params=pltpu.CompilerParams(
-            collective_id=0, has_side_effects=True, vmem_limit_bytes=56 * 2**20),
+            collective_id=0, has_side_effects=True, vmem_limit_bytes=67000000),
         name="exchange",
-    )(xt, wf, off, obs, wv)
-
-    block_rows = 16
-    slope = pl.pallas_call(
-        functools.partial(backward_kernel, block_rows, depth, channels),
+    )(layer_inputs[0], conv_weight, observed, channel_offset[None], var_weight[None])
+
+    block_rows, pitch = 16, 24
+    pred, slope = pl.pallas_call(
+        functools.partial(backward_kernel, block_rows, pitch, channels, outputs),
         grid=(rows // block_rows,),
-        out_shape=jax.ShapeDtypeStruct((channels, rows, LANES), BF),
-        in_specs=[vmem] * 4,
-        out_specs=pl.BlockSpec((channels, block_rows, LANES), lambda i: (0, i, 0)),
+        out_shape=(
+            jax.ShapeDtypeStruct((outputs, rows, LANES), BF),
+            jax.ShapeDtypeStruct((channels, rows, LANES), BF),
+        ),
+        in_specs=[vmem] * 5,
+        out_specs=(
+            pl.BlockSpec((outputs, block_rows, LANES), lambda i: (0, i, 0)),
+            pl.BlockSpec((channels, block_rows, LANES), lambda i: (0, i, 0)),
+        ),
         scratch_shapes=[
-            pltpu.VMEM((block_rows + 2, depth, LANES), BF),
-            pltpu.VMEM((channels * block_rows, LANES), F32),
+            pltpu.VMEM((block_rows + 2, channels, LANES), BF),
+            pltpu.VMEM((channels * pitch, LANES), F32),
+            pltpu.VMEM((OP * pitch, LANES), F32),
         ],
-        compiler_params=pltpu.CompilerParams(vmem_limit_bytes=56 * 2**20),
+        compiler_params=pltpu.CompilerParams(vmem_limit_bytes=67000000),
         name="backward",
-    )(grad, halo_l, halo_r, wb)
-    return pred[:, :outputs].transpose(1, 0, 2)[None], slope[None]
+    )(grad, halo_l, halo_r, wb, pred_rows)
+    return pred[None], slope[None]
 
 
 def solution(mesh):

time: 88.9 us -> 72.7 us (0.82)
  local copies, waits for them, and re-layouts: 12.4 us -> 0 us
  Pallas kernels: 75.4 us -> 72 us
    unnamed x10 -> x0, local copies, waits for them, and re-layouts: 7.34 us -> none
    pallas_call x1, Pallas kernels: 11.2 us -> 7.05 us  [shards(): pl.pallas_call(functools.partial(backward_kernel, block_rows, pitch, chan...]
    pad x5 -> x0, local copies, waits for them, and re-layouts: 2.35 us -> none  [the longest x1 1.02 us: shards(): weight = jnp.pad(conv_weight, ((0, 0), (0, 0), (0, OP - outputs), (0, 0)))]
    broadcast_in_dim x3 -> x0, local copies, waits for them, and re-layouts: 1.5 us -> none  [the longest x1 0.75 us: shards(): wv = jnp.broadcast_to(wv[:, :, None], (rounds, OP, LANES))]
    reshape x1 -> x0, local copies, waits for them, and re-layouts: 0.92 us -> none  [shards(): wb = wb.reshape(3 * depth, channels).T]
where the time goes in v2:
time: 72.7 us; the launch traced here: 72.6 us
  Pallas kernels  72 us (99%)
    pallas_call x1, Pallas kernels, shards(): pl.pallas_call(functools.partial(exchange_kernel, members, lats, lons, ro...  64.9 us
    pallas_call x1, Pallas kernels, shards(): pl.pallas_call(functools.partial(backward_kernel, block_rows, pitch, chan...  7.05 us

profile of v2, /device:TPU:2, one launch (start us, length us, event | category | flops | bytes accessed | tf_op | source)
XLA Modules:
  0.0 72.6 jit_solution(10580970779983109276)
XLA Ops:
  0.6 64.9 %exchange.1 = (bf16[48,72,128]{2,1,0:T(8,128)(2,1)}, bf16[50,72,128]{2,1,0:T(8,128)(2,1)}, bf16[72,128]{1,0:T(8,128)(2,1)}, bf16[72,128]{1,0:T(8,128)(2,1)}, bf16[256,768]{1,0:T(8,128)(2,1)}) custom-call(bf16[256,48,128]{2,1,0:T(8,128)(2,1)} %bitcast.5, bf16[3,3,69,256]{3,2,1,0:T(8,128)(2,1)} %weight.1, bf16[69,48,128]{2,1,0:T(8,128)(2,1)} %observed.1, ...), custom_call_target="tpu_custom_call" | custom-call | tf_op jit(solution)/shard_map/exchange/pallas_call | solution.py:387
  65.6 7.1 %backward.1 = (bf16[69,48,128]{2,1,0:T(8,128)(2,1)}, bf16[256,48,128]{2,1,0:T(8,128)(2,1)}) custom-call(bf16[50,72,128]{2,1,0:T(8,128)(2,1)} %get-tuple-element.9.grad, bf16[72,128]{1,0:T(8,128)(2,1)} %get-tuple-element.10.halo_l, bf16[72,128]{1,0:T(8,128)(2,1)} %get-tuple-element.11.halo_r, bf16[256,768]{1,0:T(8,128)(2,1)} %get-tuple-element.12.wb, ...), custom_call_target="tpu_custom_call" | custom-call | tf_op jit(solution)/shard_map/backward/pallas_call | solution.py:430

commit v3 on v2

--- a/solution.py
+++ b/solution.py
@@ -30,12 +30,41 @@
     return jnp.broadcast_to(jnp.sum(spread, axis=1, keepdims=True), (OP, LANES))
 
 
+def beyond_columns(grad, indices, outputs, stage):
+    last = OP - 8
+    for g in indices:
+        stage[8 * g:8 * g + 8, :] = grad[g, last:OP, :].astype(F32)
+    to_left = stage[pl.ds(outputs - last, 64, stride=8), :]
+    to_right = stage[pl.ds(outputs - last + 1, 64, stride=8), :]
+    return jnp.concatenate([to_left, to_right], axis=0).T[:OP]
+
+
+def widen(grad, g, sides, at, channels):
+    lane = lanes_of((OP, LANES))
+    row = grad[g].astype(F32)
+    right = pltpu.roll(sides, (63 - at) % LANES, 1)
+    left = sides if at == 0 else pltpu.roll(sides, LANES - at, 1)
+    after = jnp.where(lane == LANES - 1, right, pltpu.roll(row, LANES - 1, 1))
+    before = jnp.where(lane == 0, left, pltpu.roll(row, 1, 1))
+    return jnp.concatenate(
+        [after, row, before, jnp.zeros((channels - 3 * OP, LANES), F32)], axis=0).astype(BF)
+
+
+def slope_rows(wb, gs, flat, starts, shift, pitch, channels):
+    for r in starts:
+        taps = jnp.concatenate(
+            [gs[r:r + 3].reshape(3 * channels, LANES), gs[r + 1:r + 4].reshape(3 * channels, LANES)], axis=1)
+        res = jnp.dot(wb[...], taps, preferred_element_type=F32)
+        for h in range(2):
+            flat[pl.ds(r + h + shift, channels, stride=pitch), :] = res[:, h * LANES:(h + 1) * LANES]
+
+
 def exchange_kernel(
     members, lats, lons, rounds, channels, outputs,
     xn, weight, observed, offset_in, var_in,
-    pred, grad, halo_l, halo_r, wb,
-    xv, xs, stage, wv, wf, obn, obs, offset, var, off, varb, acc, edge, edge_l, edge_r, block, vals, gout, cols, cols_bf,
-    xsem, wsem, osem, smem, hsend, hrecv, esend, erecv, psend, precv, gsend, grecv, rsend, rrecv, csend, crecv,
+    pred_out, grad, wb, slope_out,
+    xv, xs, stage, wv, wf, obn, obs, offset, var, off, varb, acc, edge, edge_l, edge_r, block, vals, gout, gcol, gcol_l, gcol_r, pred, gs, flat, flat_p, pbuf, sbuf,
+    xsem, wsem, osem, smem, hsend, hrecv, esend, erecv, psend, precv, gsend, grecv, rsend, rrecv, csend, crecv, fsem,
 ):
     me = lax.axis_index("member")
     lat = lax.axis_index("lat")
@@ -147,6 +176,8 @@
                 mine = a2 if i + 64 == 0 else pltpu.roll(a2, 64 + i, 1)
                 collected = jnp.where(lane == 64 + i, mine, collected)
         edge[s] = collected
+
+    def send_edges(s):
         edge_copy(s, right, edge_l, 0).start()
         edge_copy(s, left, edge_r, 1).start()
 
@@ -192,8 +223,9 @@
     off[...] = column(offset[...], outputs)
     for j in blocks[:4]:
         relay(j)
+    convolve(1)
     pl.semaphore_wait(barrier, members - 1 + 2 + has_up.astype(jnp.int32) + has_down.astype(jnp.int32))
-    convolve(1)
+    send_edges(1)
     relay(0)
     relay(5)
     @pl.when(has_up)
@@ -203,6 +235,7 @@
     @pl.when(has_down)
     def _():
         row_down().start()
+
     for t in range(3):
         taps = [wv[2 - t, b].astype(F32) for b in range(3)]
         pad = jnp.zeros((OP - outputs, channels), F32)
@@ -216,12 +249,14 @@
         row_down().wait_recv()
 
     convolve(0)
+    send_edges(0)
 
     @pl.when(has_down)
     def _():
         row_up().wait_recv()
 
     convolve(2)
+    send_edges(2)
     finish(0)
     finish(2)
 
@@ -234,6 +269,11 @@
         buf[0:8 * outputs, :] = obn[s].astype(F32).reshape(8 * outputs, LANES)
         picked = buf[pl.ds(lax.rem(me, 8), OP, stride=8), :]
         obs[s] = jnp.where(variable < outputs, picked, 0.0)
+
+    def col_copy(s, side, dst, k):
+        return pltpu.make_async_remote_copy(
+            gcol.at[s], dst.at[s], csend.at[s, k], crecv.at[s, k],
+            device_id=(me, lat, side), device_id_type=MESH)
 
     def grad_copy(s, d, to):
         other = lax.rem(me + d, members) if to else lax.rem(me + members - d, members)
@@ -267,6 +307,22 @@
             return carry
 
         lax.fori_loop(0, OP // 8, slab, 0)
+        collected = jnp.zeros((OP, LANES), F32)
+        for j in range(members):
+            first = vals[j] if j == 0 else pltpu.roll(vals[j], j, 1)
+            collected = jnp.where(lane == j, first, collected)
+            collected = jnp.where(lane == 64 + j, pltpu.roll(vals[j], 65 + j, 1), collected)
+        gcol[s] = collected.astype(BF)
+        col_copy(s, right, gcol_l, 0).start()
+        col_copy(s, left, gcol_r, 1).start()
+        col_copy(s, right, gcol_l, 0).wait_recv()
+        col_copy(s, left, gcol_r, 1).wait_recv()
+        both = jnp.where(
+            lane < 64, pltpu.roll(gcol_l[s].astype(F32), 64, 1), pltpu.roll(gcol_r[s].astype(F32), 64, 1))
+        across = jnp.concatenate([both, jnp.zeros((LANES - OP, LANES), F32)], axis=0).T
+        for j in range(members):
+            vals[j, outputs:outputs + 1, :] = across[j:j + 1]
+            vals[j, outputs + 1:outputs + 2, :] = across[64 + j:65 + j]
         gout[s] = vals[...].astype(BF)
 
         def send(d, carry):
@@ -276,55 +332,66 @@
         lax.fori_loop(1, members, send, 0)
         grad[1 + members * s + me] = gout[s, me]
 
-    def collect(g):
-        row = grad[g].astype(F32)
-        now = jnp.where(lane == g, pltpu.roll(row, g, 1), cols[...])
-        cols[...] = jnp.where(lane == 64 + g, pltpu.roll(row, 65 + g, 1), now)
-
-    cols[...] = jnp.zeros_like(cols)
-    for s in (0, 2, 1):
+    def return_of(s):
         def arrive_back(d, carry):
             grad_copy(s, d, False).wait_recv()
             return carry
 
         lax.fori_loop(1, members, arrive_back, 0)
-        if s == 0:
-            @pl.when(has_up)
-            def _():
-                grow_up().start()
-        if s == 2:
-            @pl.when(has_down)
-            def _():
-                grow_down().start()
-
-        def gather(i, carry):
-            collect(1 + members * s + i)
-            return carry
-
-        lax.fori_loop(0, members, gather, 0)
+
+    def pred_part(s):
+        for i in range(members):
+            flat_p[pl.ds(i, OP, stride=24), :] = pred[members * s + i].astype(F32)
+        pbuf[s] = flat_p[...].reshape(OP, 24, LANES)[:outputs, :members].astype(BF)
+
+    def pred_done(s):
+        return pltpu.make_async_copy(pbuf.at[s], pred_out.at[:, pl.ds(members * s, members), :], fsem.at[s])
+
+    for s in range(rounds):
+        pred_part(s)
+        pred_done(s).start()
+
+    return_of(0)
 
     @pl.when(has_up)
     def _():
+        grow_up().start()
+
+    return_of(2)
+
+    @pl.when(has_down)
+    def _():
+        grow_down().start()
+
+    @pl.when(has_up)
+    def _():
         grow_down().wait_recv()
 
     @pl.when(has_down)
     def _():
         grow_up().wait_recv()
 
-    collect(0)
-    collect(rows + 1)
-    cols_bf[...] = cols[...].astype(BF)
-
-    def col_copy(side, dst, k):
-        return pltpu.make_async_remote_copy(
-            cols_bf, dst, csend.at[k], crecv.at[k], device_id=(me, lat, side), device_id_type=MESH)
-
-    col_copy(right, halo_l, 0).start()
-    col_copy(left, halo_r, 1).start()
+    def slope_copy(k):
+        return pltpu.make_async_copy(
+            sbuf.at[k], slope_out.at[:, pl.ds(2 * members * k, members), :], fsem.at[rounds + k])
+
+    early = (range(0, members + 1), range(2 * members + 1, rows + 2))
+    sides = beyond_columns(grad, [*early[0], *early[1]], outputs, stage.at[0])
+    starts = [*range(0, members - 3, 2), members - 3]
+    for k, part in enumerate(early):
+        for i, g in enumerate(part):
+            gs[k, i] = widen(grad, g, sides, g, channels)
+        slope_rows(wb, gs.at[k], flat.at[k], starts, k, 24, channels)
+        sbuf[k] = flat[k].reshape(channels, 24, LANES)[:, :members].astype(BF)
+        slope_copy(k).start()
+
+    return_of(1)
 
     for s in range(rounds):
         edge_copy(s, right, edge_l, 0).wait_send()
         edge_copy(s, left, edge_r, 1).wait_send()
+        col_copy(s, right, gcol_l, 0).wait_send()
+        col_copy(s, left, gcol_r, 1).wait_send()
 
         def left_device(d, carry):
             pred_copy(s, d, True).wait_send()
@@ -343,36 +410,60 @@
         row_down().wait_send()
         grow_down().wait_send()
 
-    col_copy(right, halo_l, 0).wait()
-    col_copy(left, halo_r, 1).wait()
+    for s in range(rounds):
+        pred_done(s).wait()
+    for k in range(2):
+        slope_copy(k).wait()
 
 
 def backward_kernel(
-    block_rows, pitch, channels, outputs, grad, halo_l, halo_r, wb, rows_in, pred, slope, gs, flat, flat_p
+    members, channels, outputs, grad_in, wb_in, slope_in, pred_in, pred, slope,
+    grad, wb, blocks, pbuf, gs, flat, stage, isem, osem,
 ):
-    step = pl.program_id(0)
-    lane = lanes_of((OP, LANES))
-    first = step * block_rows
-    hl = halo_l[...].astype(F32)
-    hr = halo_r[...].astype(F32)
-    for i in range(block_rows + 2):
-        g = first + i
-        row = grad[g].astype(F32)
-        after = jnp.where(lane == LANES - 1, pltpu.roll(hr, LANES - 1 - g, 1), pltpu.roll(row, LANES - 1, 1))
-        before = jnp.where(lane == 0, pltpu.roll(hl, lax.rem(LANES + 64 - g, LANES), 1), pltpu.roll(row, 1, 1))
-        full = jnp.concatenate([after, row, before, jnp.zeros((channels - 3 * OP, LANES), F32)], axis=0)
-        gs[i] = full.astype(BF)
-    for i in range(block_rows):
-        flat_p[pl.ds(i, OP, stride=pitch), :] = rows_in[first + i].astype(F32)
-    pred[...] = flat_p[...].reshape(OP, pitch, LANES)[:outputs, :block_rows].astype(BF)
-    for q in range(block_rows // 2):
-        r = 2 * q
-        taps = jnp.concatenate(
-            [gs[r:r + 3].reshape(3 * channels, LANES), gs[r + 1:r + 4].reshape(3 * channels, LANES)], axis=1)
-        res = jnp.dot(wb[...], taps, preferred_element_type=F32)
-        for h in range(2):
-            flat[pl.ds(r + h, channels, stride=pitch), :] = res[:, h * LANES:(h + 1) * LANES]
-    slope[...] = flat[...].reshape(channels, pitch, LANES)[:, :block_rows].astype(BF)
+    count = members + 4
+    first = members - 1
+    pitch = 2 * members + 8
+    ins = [
+        pltpu.make_async_copy(grad_in.at[pl.ds(first, count)], grad, isem.at[0]),
+        pltpu.make_async_copy(wb_in, wb, isem.at[1]),
+    ]
+    block_at = (0, 1, 4, 5)
+    for k, j in enumerate(block_at):
+        ins.append(pltpu.make_async_copy(slope_in.at[:, pl.ds(8 * j, 8), :], blocks.at[j], isem.at[2 + k]))
+    ins.append(pltpu.make_async_copy(pred_in, pbuf, isem.at[6]))
+    for c in ins:
+        c.start()
+
+    def out_copy(j):
+        return pltpu.make_async_copy(blocks.at[j], slope.at[:, pl.ds(8 * j, 8), :], osem.at[j])
+
+    pred_copy = pltpu.make_async_copy(pbuf, pred, osem.at[6])
+    ins[0].wait()
+    sides = beyond_columns(grad, range(count), outputs, stage)
+    for i in range(count):
+        gs[i] = widen(grad, i, sides, i, channels)
+    ins[1].wait()
+    for k, j in ((2, 0), (5, 5)):
+        ins[k].wait()
+        out_copy(j).start()
+    ins[6].wait()
+    pred_copy.start()
+    slope_rows(wb, gs, flat, range(0, members + 2, 2), 7, pitch, channels)
+    ins[3].wait()
+    ins[4].wait()
+    area = (channels, 8, LANES)
+    row = lax.broadcasted_iota(jnp.int32, area, 1)
+    new = flat[...].reshape(channels, pitch, LANES)
+    for j in (2, 3):
+        blocks[j] = new[:, 8 * j - 8:8 * j].astype(BF)
+        out_copy(j).start()
+    blocks[1] = jnp.where(row == 7, new[:, 0:8], blocks[1].astype(F32)).astype(BF)
+    out_copy(1).start()
+    blocks[4] = jnp.where(row == 0, new[:, 24:32], blocks[4].astype(F32)).astype(BF)
+    out_copy(4).start()
+    for j in range(6):
+        out_copy(j).wait()
+    pred_copy.wait()
 
 
 def shards(members, lats, lons, layer_inputs, conv_weight, channel_offset, observed, var_weight):
@@ -384,17 +475,16 @@
     hbm = pl.BlockSpec(memory_space=pltpu.HBM)
     dma = pltpu.SemaphoreType.DMA
     per_member = dma((rounds, members))
-    pred_rows, grad, halo_l, halo_r, wb = pl.pallas_call(
+    pred_a, grad, wb, slope_a = pl.pallas_call(
         functools.partial(exchange_kernel, members, lats, lons, rounds, channels, outputs),
         out_shape=(
-            jax.ShapeDtypeStruct((rows, OP, LANES), BF),
+            jax.ShapeDtypeStruct((outputs, rows, LANES), BF),
             jax.ShapeDtypeStruct((rows + 2, OP, LANES), BF),
-            jax.ShapeDtypeStruct((OP, LANES), BF),
-            jax.ShapeDtypeStruct((OP, LANES), BF),
             jax.ShapeDtypeStruct((channels, 3 * channels), BF),
+            jax.ShapeDtypeStruct((channels, rows, LANES), BF),
         ),
         in_specs=[hbm] * 5,
-        out_specs=(vmem,) * 5,
+        out_specs=(hbm, vmem, vmem, hbm),
         scratch_shapes=[
             pltpu.VMEM((rows // 8, channels, 8, LANES), BF),
             pltpu.VMEM((rows + 2, channels, LANES), BF),
@@ -414,39 +504,46 @@
             pltpu.VMEM((rounds, members, OP, LANES), BF),
             pltpu.VMEM((members, OP, LANES), F32),
             pltpu.VMEM((rounds, members, OP, LANES), BF),
-            pltpu.VMEM((OP, LANES), F32),
-            pltpu.VMEM((OP, LANES), BF),
+            pltpu.VMEM((rounds, OP, LANES), BF),
+            pltpu.VMEM((rounds, OP, LANES), BF),
+            pltpu.VMEM((rounds, OP, LANES), BF),
+            pltpu.VMEM((rows, OP, LANES), BF),
+            pltpu.VMEM((2, members + 2, channels, LANES), BF),
+            pltpu.VMEM((2, channels * 24, LANES), F32),
+            pltpu.VMEM((OP * 24, LANES), F32),
+            pltpu.VMEM((rounds, outputs, members, LANES), BF),
+            pltpu.VMEM((2, channels, members, LANES), BF),
             dma((rows // 8,)), dma, dma((rounds,)), dma((2,)),
             dma((2,)), dma((2,)), dma((rounds, 2)), dma((rounds, 2)),
             per_member, per_member, per_member, per_member,
-            dma((2,)), dma((2,)), dma((2,)), dma((2,)),
+            dma((2,)), dma((2,)), dma((rounds, 2)), dma((rounds, 2)), dma((rounds + 2,)),
         ],
         compiler_params=pltpu.CompilerParams(
             collective_id=0, has_side_effects=True, vmem_limit_bytes=67000000),
         name="exchange",
     )(layer_inputs[0], conv_weight, observed, channel_offset[None], var_weight[None])
 
-    block_rows, pitch = 16, 24
     pred, slope = pl.pallas_call(
-        functools.partial(backward_kernel, block_rows, pitch, channels, outputs),
-        grid=(rows // block_rows,),
+        functools.partial(backward_kernel, members, channels, outputs),
         out_shape=(
             jax.ShapeDtypeStruct((outputs, rows, LANES), BF),
             jax.ShapeDtypeStruct((channels, rows, LANES), BF),
         ),
-        in_specs=[vmem] * 5,
-        out_specs=(
-            pl.BlockSpec((outputs, block_rows, LANES), lambda i: (0, i, 0)),
-            pl.BlockSpec((channels, block_rows, LANES), lambda i: (0, i, 0)),
-        ),
+        in_specs=[hbm] * 4,
+        out_specs=(hbm, hbm),
         scratch_shapes=[
-            pltpu.VMEM((block_rows + 2, channels, LANES), BF),
-            pltpu.VMEM((channels * pitch, LANES), F32),
-            pltpu.VMEM((OP * pitch, LANES), F32),
+            pltpu.VMEM((members + 4, OP, LANES), BF),
+            pltpu.VMEM((channels, 3 * channels), BF),
+            pltpu.VMEM((rows // 8, channels, 8, LANES), BF),
+            pltpu.VMEM((outputs, rows, LANES), BF),
+            pltpu.VMEM((members + 4, channels, LANES), BF),
+            pltpu.VMEM((channels * (2 * members + 8), LANES), F32),
+            pltpu.VMEM((8 * 64, LANES), F32),
+            dma((7,)), dma((7,)),
         ],
         compiler_params=pltpu.CompilerParams(vmem_limit_bytes=67000000),
         name="backward",
-    )(grad, halo_l, halo_r, wb, pred_rows)
+    )(grad, wb, slope_a, pred_a)
     return pred[None], slope[None]
 
 

time: 72.7 us -> 69 us (0.949)
  the two profiles are of different devices: /device:TPU:2 before, /device:TPU:1 now
where the time goes in v3:
time: 69 us; the launch traced here: 68.9 us
  Pallas kernels  68.2 us (99%)
    pallas_call x1, Pallas kernels, shards(): pl.pallas_call(functools.partial(exchange_kernel, members, lats, lons, ro...  63.5 us
    pallas_call x1, Pallas kernels, shards(): pl.pallas_call(functools.partial(backward_kernel, members, channels, outp...  4.74 us

profile of v3, /device:TPU:1, one launch (start us, length us, event | category | flops | bytes accessed | tf_op | source)
XLA Modules:
  0.0 68.9 jit_solution(5388874625348431566)
XLA Ops:
  0.6 63.5 %exchange.1 = (bf16[69,48,128]{2,1,0:T(8,128)(2,1)}, bf16[50,72,128]{2,1,0:T(8,128)(2,1)}, bf16[256,768]{1,0:T(8,128)(2,1)}, bf16[256,48,128]{2,1,0:T(8,128)(2,1)}) custom-call(bf16[256,48,128]{2,1,0:T(8,128)(2,1)} %bitcast.5, bf16[3,3,69,256]{3,2,1,0:T(8,128)(2,1)} %weight.1, bf16[69,48,128]{2,1,0:T(8,128)(2,1)} %observed.1, f32[1,69]{1,0:T(1,128)} %bitcast.6, ...), custom_call_target="tpu_custom_call" | custom-call | tf_op jit(solution)/shard_map/exchange/pallas_call | solution.py:478
  64.1 4.7 %backward.1 = (bf16[69,48,128]{2,1,0:T(8,128)(2,1)}, bf16[256,48,128]{2,1,0:T(8,128)(2,1)}) custom-call(bf16[50,72,128]{2,1,0:T(8,128)(2,1)} %get-tuple-element.8.grad_in, bf16[256,768]{1,0:T(8,128)(2,1)} %get-tuple-element.9.wb_in, bf16[256,48,128]{2,1,0:T(8,128)(2,1)} %get-tuple-element.10.slope_in, bf16[69,48,128]{2,1,0:T(8,128)(2,1)} %get-tuple-element.11.pred_in), custom_call_target="tpu_custom_call" | custom-call | tf_op jit(solution)/shard_map/backward/pallas_call | solution.py:526

commit v4 on v3

--- a/solution.py
+++ b/solution.py
@@ -22,6 +22,25 @@
 
 def lanes_of(shape):
     return lax.broadcasted_iota(jnp.int32, shape, len(shape) - 1)
+
+
+def rounds_of(members, rows):
+    m = members
+    return (
+        [*range(1, m - 1), 2 * m + 1, 2 * m + 2],
+        [0, m - 1, 2 * m, *range(2 * m + 3, rows)],
+        [*range(m, 2 * m)],
+    )
+
+
+def row_at(plan, s, owner):
+    listed, members = plan[s], len(plan[s])
+    row = owner + listed[0]
+    for k in range(1, members):
+        jump = listed[k] - listed[k - 1] - 1
+        if jump:
+            row = row + jump * ((owner + members - k) // members)
+    return row
 
 
 def column(vector, count):
@@ -62,9 +81,9 @@
 def exchange_kernel(
     members, lats, lons, rounds, channels, outputs,
     xn, weight, observed, offset_in, var_in,
-    pred_out, grad, wb, slope_out,
-    xv, xs, stage, wv, wf, obn, obs, offset, var, off, varb, acc, edge, edge_l, edge_r, block, vals, gout, gcol, gcol_l, gcol_r, pred, gs, flat, flat_p, pbuf, sbuf,
-    xsem, wsem, osem, smem, hsend, hrecv, esend, erecv, psend, precv, gsend, grecv, rsend, rrecv, csend, crecv, fsem,
+    pred_out, grad_out, wb_out, slope_out,
+    xv, xs, stage, wv, wf, obn, obs, offset, var, off, varb, acc, edge, edge_l, edge_r, block, vals_of, gout, gcol, gcol_l, gcol_r, pred, gs, flat, flat_p, pbuf, sbuf, grad, wb,
+    xsem, wsem, osem, smem, hsend, hrecv, esend, erecv, psend, precv, gsend, grecv, rsend, rrecv, csend, crecv, fsem, ready,
 ):
     me = lax.axis_index("member")
     lat = lax.axis_index("lat")
@@ -74,7 +93,9 @@
     rows = rounds * members
     has_up = lat > 0
     has_down = lat < lats - 1
-    blocks = (2, 3, 1, 4, 0, 5)
+    plan = rounds_of(members, rows)
+    blocks = (0, 1, 4, 2, 3, 5)
+    mine = [row_at(plan, s, me) for s in range(rounds)]
 
     def block_copy(j):
         return pltpu.make_async_copy(xn.at[:, pl.ds(8 * j, 8), :], xv.at[j], xsem.at[j])
@@ -83,7 +104,7 @@
         return pltpu.make_async_copy(weight, wv, wsem)
 
     def observed_copy(s):
-        start = pl.multiple_of(members * s + 8 * (me // 8), 8)
+        start = pl.multiple_of(8 * (mine[s] // 8), 8)
         return pltpu.make_async_copy(observed.at[:, pl.ds(start, 8), :], obn.at[s], osem.at[s])
 
     def small_copy(k):
@@ -101,13 +122,16 @@
 
     barrier = pltpu.get_barrier_semaphore()
 
-    def greet(d, carry):
+    side_len = math.isqrt(members)
+    own_col, own_row = me // side_len, lax.rem(me, side_len)
+
+    def in_row(d):
+        return (own_col * side_len + lax.rem(own_row + d, side_len), lat, lon)
+
+    for d in range(1, side_len):
+        pl.semaphore_signal(barrier, inc=1, device_id=in_row(d), device_id_type=MESH)
         pl.semaphore_signal(
-            barrier, inc=1, device_id=(lax.rem(me + d, members), lat, lon), device_id_type=MESH
-        )
-        return carry
-
-    lax.fori_loop(1, members, greet, 0)
+            barrier, inc=1, device_id=(lax.rem(me + d * side_len, members), lat, lon), device_id_type=MESH)
     for side in (left, right):
         pl.semaphore_signal(barrier, inc=1, device_id=(me, lat, side), device_id_type=MESH)
 
@@ -159,10 +183,8 @@
     def convolve(s):
         collected = jnp.zeros((OP, LANES), F32)
         for q in range(members // 2):
-            r = members * s + 2 * q
             taps = jnp.concatenate(
-                [xs[r:r + 3].reshape(3 * channels, LANES), xs[r + 1:r + 4].reshape(3 * channels, LANES)],
-                axis=1)
+                [xs[r:r + 3].reshape(3 * channels, LANES) for r in plan[s][2 * q:2 * q + 2]], axis=1)
             res = jnp.dot(wf[...], taps, preferred_element_type=F32)
             for h in range(2):
                 i = 2 * q + h
@@ -221,13 +243,16 @@
             wf[b * OP:(b + 1) * OP, a * channels:(a + 1) * channels] = full.astype(BF)
     small_copy(0).wait()
     off[...] = column(offset[...], outputs)
-    for j in blocks[:4]:
+    for j in blocks[:3]:
         relay(j)
-    convolve(1)
-    pl.semaphore_wait(barrier, members - 1 + 2 + has_up.astype(jnp.int32) + has_down.astype(jnp.int32))
-    send_edges(1)
-    relay(0)
-    relay(5)
+    convolve(0)
+    pl.semaphore_wait(barrier, 2 * (side_len - 1) + 2 + has_up.astype(jnp.int32) + has_down.astype(jnp.int32))
+    for d in range(1, side_len):
+        pl.semaphore_signal(ready, inc=1, device_id=in_row(d), device_id_type=MESH)
+
+    send_edges(0)
+    for j in blocks[3:]:
+        relay(j)
     @pl.when(has_up)
     def _():
         row_up().start()
@@ -242,22 +267,22 @@
         tall = jnp.concatenate(
             [taps[0], pad, taps[1], pad, taps[2], pad, jnp.zeros((channels - 3 * OP, channels), F32)], axis=0)
         wb[:, t * channels:(t + 1) * channels] = tall.T.astype(BF)
-    finish(1)
+    pl.semaphore_wait(ready, side_len - 1)
+    finish(0)
 
     @pl.when(has_up)
     def _():
         row_down().wait_recv()
 
-    convolve(0)
-    send_edges(0)
-
     @pl.when(has_down)
     def _():
         row_up().wait_recv()
 
+    convolve(1)
+    send_edges(1)
     convolve(2)
     send_edges(2)
-    finish(0)
+    finish(1)
     finish(2)
 
     small_copy(1).wait()
@@ -267,7 +292,7 @@
         observed_copy(s).wait()
         buf = stage.at[s % 2]
         buf[0:8 * outputs, :] = obn[s].astype(F32).reshape(8 * outputs, LANES)
-        picked = buf[pl.ds(lax.rem(me, 8), OP, stride=8), :]
+        picked = buf[pl.ds(lax.rem(mine[s], 8), OP, stride=8), :]
         obs[s] = jnp.where(variable < outputs, picked, 0.0)
 
     def col_copy(s, side, dst, k):
@@ -279,17 +304,29 @@
         other = lax.rem(me + d, members) if to else lax.rem(me + members - d, members)
         owner = me if to else other
         return pltpu.make_async_remote_copy(
-            gout.at[s, other], grad.at[1 + members * s + owner], gsend.at[s, d], grecv.at[s, owner],
+            gout.at[s, other], grad.at[1 + row_at(plan, s, owner)], gsend.at[s, d], grecv.at[s, owner],
             device_id=(other, lat, lon), device_id_type=MESH)
 
-    for s in (0, 2, 1):
+    where = {row: members * s + i for s in range(rounds) for i, row in enumerate(plan[s])}
+
+    def pred_part(s):
+        for i in range(members):
+            flat_p[pl.ds(i, OP, stride=24), :] = pred[where[members * s + i]].astype(F32)
+        pbuf[s] = flat_p[...].reshape(OP, 24, LANES)[:outputs, :members].astype(BF)
+
+    def pred_done(s):
+        return pltpu.make_async_copy(pbuf.at[s], pred_out.at[:, pl.ds(members * s, members), :], fsem.at[s])
+
+    def arrive_stage(s):
         def arrive(d, carry):
             pred_copy(s, d, False).wait_recv()
             return carry
 
         lax.fori_loop(1, members, arrive, 0)
+    def pair_stage(s):
+        vals = vals_of.at[s]
         vals[...] = block[s].astype(F32)
-        row_index = jnp.full((8, LANES), lat * rows + members * s + me, jnp.int32).astype(F32)
+        row_index = jnp.full((8, LANES), lat * rows + mine[s], jnp.int32).astype(F32)
         angle = -80.0 + 160.0 * (row_index + 0.5) / float(rows * lats)
         lat_weight = jnp.cos(angle * (math.pi / 180.0))
 
@@ -315,6 +352,11 @@
         gcol[s] = collected.astype(BF)
         col_copy(s, right, gcol_l, 0).start()
         col_copy(s, left, gcol_r, 1).start()
+
+    def return_stage(s):
+        vals = vals_of.at[s]
+        pred_part(s)
+        pred_done(s).start()
         col_copy(s, right, gcol_l, 0).wait_recv()
         col_copy(s, left, gcol_r, 1).wait_recv()
         both = jnp.where(
@@ -330,7 +372,17 @@
             return carry
 
         lax.fori_loop(1, members, send, 0)
-        grad[1 + members * s + me] = gout[s, me]
+        grad[1 + mine[s]] = gout[s, me]
+
+    arrive_stage(0)
+    pair_stage(0)
+    arrive_stage(1)
+    pair_stage(1)
+    arrive_stage(2)
+    return_stage(0)
+    pair_stage(2)
+    return_stage(1)
+    return_stage(2)
 
     def return_of(s):
         def arrive_back(d, carry):
@@ -339,25 +391,14 @@
 
         lax.fori_loop(1, members, arrive_back, 0)
 
-    def pred_part(s):
-        for i in range(members):
-            flat_p[pl.ds(i, OP, stride=24), :] = pred[members * s + i].astype(F32)
-        pbuf[s] = flat_p[...].reshape(OP, 24, LANES)[:outputs, :members].astype(BF)
-
-    def pred_done(s):
-        return pltpu.make_async_copy(pbuf.at[s], pred_out.at[:, pl.ds(members * s, members), :], fsem.at[s])
-
-    for s in range(rounds):
-        pred_part(s)
-        pred_done(s).start()
-
+    wb_done = pltpu.make_async_copy(wb, wb_out, fsem.at[rounds + 3])
+    wb_done.start()
     return_of(0)
+    return_of(1)
 
     @pl.when(has_up)
     def _():
         grow_up().start()
-
-    return_of(2)
 
     @pl.when(has_down)
     def _():
@@ -385,7 +426,10 @@
         sbuf[k] = flat[k].reshape(channels, 24, LANES)[:, :members].astype(BF)
         slope_copy(k).start()
 
-    return_of(1)
+    return_of(2)
+    grad_done = pltpu.make_async_copy(
+        grad.at[pl.ds(members - 1, members + 4)], grad_out, fsem.at[rounds + 2])
+    grad_done.start()
 
     for s in range(rounds):
         edge_copy(s, right, edge_l, 0).wait_send()
@@ -414,6 +458,8 @@
         pred_done(s).wait()
     for k in range(2):
         slope_copy(k).wait()
+    wb_done.wait()
+    grad_done.wait()
 
 
 def backward_kernel(
@@ -421,10 +467,9 @@
     grad, wb, blocks, pbuf, gs, flat, stage, isem, osem,
 ):
     count = members + 4
-    first = members - 1
     pitch = 2 * members + 8
     ins = [
-        pltpu.make_async_copy(grad_in.at[pl.ds(first, count)], grad, isem.at[0]),
+        pltpu.make_async_copy(grad_in, grad, isem.at[0]),
         pltpu.make_async_copy(wb_in, wb, isem.at[1]),
     ]
     block_at = (0, 1, 4, 5)
@@ -448,18 +493,23 @@
         out_copy(j).start()
     ins[6].wait()
     pred_copy.start()
-    slope_rows(wb, gs, flat, range(0, members + 2, 2), 7, pitch, channels)
-    ins[3].wait()
-    ins[4].wait()
     area = (channels, 8, LANES)
     row = lax.broadcasted_iota(jnp.int32, area, 1)
-    new = flat[...].reshape(channels, pitch, LANES)
-    for j in (2, 3):
-        blocks[j] = new[:, 8 * j - 8:8 * j].astype(BF)
-        out_copy(j).start()
-    blocks[1] = jnp.where(row == 7, new[:, 0:8], blocks[1].astype(F32)).astype(BF)
+
+    def computed(j):
+        return flat[...].reshape(channels, pitch, LANES)[:, 8 * j - 8:8 * j]
+
+    slope_rows(wb, gs, flat, range(0, 10, 2), 7, pitch, channels)
+    blocks[2] = computed(2).astype(BF)
+    out_copy(2).start()
+    ins[3].wait()
+    blocks[1] = jnp.where(row == 7, computed(1), blocks[1].astype(F32)).astype(BF)
     out_copy(1).start()
-    blocks[4] = jnp.where(row == 0, new[:, 24:32], blocks[4].astype(F32)).astype(BF)
+    slope_rows(wb, gs, flat, range(10, members + 2, 2), 7, pitch, channels)
+    blocks[3] = computed(3).astype(BF)
+    out_copy(3).start()
+    ins[4].wait()
+    blocks[4] = jnp.where(row == 0, computed(4), blocks[4].astype(F32)).astype(BF)
     out_copy(4).start()
     for j in range(6):
         out_copy(j).wait()
@@ -471,7 +521,6 @@
     outputs = conv_weight.shape[2]
     rounds = rows // members
 
-    vmem = pl.BlockSpec(memory_space=pltpu.VMEM)
     hbm = pl.BlockSpec(memory_space=pltpu.HBM)
     dma = pltpu.SemaphoreType.DMA
     per_member = dma((rounds, members))
@@ -479,12 +528,12 @@
         functools.partial(exchange_kernel, members, lats, lons, rounds, channels, outputs),
         out_shape=(
             jax.ShapeDtypeStruct((outputs, rows, LANES), BF),
-            jax.ShapeDtypeStruct((rows + 2, OP, LANES), BF),
+            jax.ShapeDtypeStruct((members + 4, OP, LANES), BF),
             jax.ShapeDtypeStruct((channels, 3 * channels), BF),
             jax.ShapeDtypeStruct((channels, rows, LANES), BF),
         ),
         in_specs=[hbm] * 5,
-        out_specs=(hbm, vmem, vmem, hbm),
+        out_specs=(hbm,) * 4,
         scratch_shapes=[
             pltpu.VMEM((rows // 8, channels, 8, LANES), BF),
             pltpu.VMEM((rows + 2, channels, LANES), BF),
@@ -502,7 +551,7 @@
             pltpu.VMEM((rounds, OP, LANES), F32),
             pltpu.VMEM((rounds, OP, LANES), F32),
             pltpu.VMEM((rounds, members, OP, LANES), BF),
-            pltpu.VMEM((members, OP, LANES), F32),
+            pltpu.VMEM((rounds, members, OP, LANES), F32),
             pltpu.VMEM((rounds, members, OP, LANES), BF),
             pltpu.VMEM((rounds, OP, LANES), BF),
             pltpu.VMEM((rounds, OP, LANES), BF),
@@ -513,10 +562,12 @@
             pltpu.VMEM((OP * 24, LANES), F32),
             pltpu.VMEM((rounds, outputs, members, LANES), BF),
             pltpu.VMEM((2, channels, members, LANES), BF),
+            pltpu.VMEM((rows + 2, OP, LANES), BF),
+            pltpu.VMEM((channels, 3 * channels), BF),
             dma((rows // 8,)), dma, dma((rounds,)), dma((2,)),
             dma((2,)), dma((2,)), dma((rounds, 2)), dma((rounds, 2)),
             per_member, per_member, per_member, per_member,
-            dma((2,)), dma((2,)), dma((rounds, 2)), dma((rounds, 2)), dma((rounds + 2,)),
+            dma((2,)), dma((2,)), dma((rounds, 2)), dma((rounds, 2)), dma((rounds + 4,)), pltpu.SemaphoreType.REGULAR,
         ],
         compiler_params=pltpu.CompilerParams(
             collective_id=0, has_side_effects=True, vmem_limit_bytes=67000000),

time: 69 us -> 67.9 us (0.984)
  Pallas kernels: 68.2 us -> 67.2 us
    pallas_call x1, Pallas kernels: 63.5 us -> 62.3 us  [shards(): pl.pallas_call(functools.partial(exchange_kernel, members, lats, lons, ro...]
where the time goes in v4:
time: 67.9 us; the launch traced here: 67.8 us
  Pallas kernels  67.2 us (99%)
    pallas_call x1, Pallas kernels, shards(): pl.pallas_call(functools.partial(exchange_kernel, members, lats, lons, ro...  62.3 us
    pallas_call x1, Pallas kernels, shards(): pl.pallas_call(functools.partial(backward_kernel, members, channels, outp...  4.85 us

profile of v4, /device:TPU:1, one launch (start us, length us, event | category | flops | bytes accessed | tf_op | source)
XLA Modules:
  0.0 67.8 jit_solution(11335986298729248962)
XLA Ops:
  0.6 62.3 %exchange.1 = (bf16[69,48,128]{2,1,0:T(8,128)(2,1)}, bf16[20,72,128]{2,1,0:T(8,128)(2,1)}, bf16[256,768]{1,0:T(8,128)(2,1)}, bf16[256,48,128]{2,1,0:T(8,128)(2,1)}) custom-call(bf16[256,48,128]{2,1,0:T(8,128)(2,1)} %bitcast.5, bf16[3,3,69,256]{3,2,1,0:T(8,128)(2,1)} %weight.1, bf16[69,48,128]{2,1,0:T(8,128)(2,1)} %observed.1, f32[1,69]{1,0:T(1,128)} %bitcast.6, ...), custom_call_target="tpu_custom_call" | custom-call | tf_op jit(solution)/shard_map/exchange/pallas_call | solution.py:527
  62.9 4.9 %backward.1 = (bf16[69,48,128]{2,1,0:T(8,128)(2,1)}, bf16[256,48,128]{2,1,0:T(8,128)(2,1)}) custom-call(bf16[20,72,128]{2,1,0:T(8,128)(2,1)} %get-tuple-element.8.grad_in, bf16[256,768]{1,0:T(8,128)(2,1)} %get-tuple-element.9.wb_in, bf16[256,48,128]{2,1,0:T(8,128)(2,1)} %get-tuple-element.10.slope_in, bf16[69,48,128]{2,1,0:T(8,128)(2,1)} %get-tuple-element.11.pred_in), custom_call_target="tpu_custom_call" | custom-call | tf_op jit(solution)/shard_map/backward/pallas_call | solution.py:577

commit v5 on v4

--- a/solution.py
+++ b/solution.py
@@ -343,7 +343,7 @@
             vals[:, part, :] = scale * (smooth(v - obs[s, part, :]) - total / (members - 1))
             return carry
 
-        lax.fori_loop(0, OP // 8, slab, 0)
+        lax.fori_loop(0, OP // 8, slab, 0, unroll=3)
         collected = jnp.zeros((OP, LANES), F32)
         for j in range(members):
             first = vals[j] if j == 0 else pltpu.roll(vals[j], j, 1)

time: 67.9 us -> 67.9 us (level)
  no operation moved by 1% of the time
where the time goes in v5:
time: 67.9 us; the launch traced here: 67.8 us
  Pallas kernels  67 us (99%)
  between operations  0.8 us (1%)
    pallas_call x1, Pallas kernels, shards(): pl.pallas_call(functools.partial(exchange_kernel, members, lats, lons, ro...  62.2 us
    pallas_call x1, Pallas kernels, shards(): pl.pallas_call(functools.partial(backward_kernel, members, channels, outp...  4.85 us

profile of v5, /device:TPU:1, one launch (start us, length us, event | category | flops | bytes accessed | tf_op | source)
XLA Modules:
  0.0 67.8 jit_solution(6302297265778456101)
XLA Ops:
  0.6 62.2 %exchange.1 = (bf16[69,48,128]{2,1,0:T(8,128)(2,1)}, bf16[20,72,128]{2,1,0:T(8,128)(2,1)}, bf16[256,768]{1,0:T(8,128)(2,1)}, bf16[256,48,128]{2,1,0:T(8,128)(2,1)}) custom-call(bf16[256,48,128]{2,1,0:T(8,128)(2,1)} %bitcast.5, bf16[3,3,69,256]{3,2,1,0:T(8,128)(2,1)} %weight.1, bf16[69,48,128]{2,1,0:T(8,128)(2,1)} %observed.1, f32[1,69]{1,0:T(1,128)} %bitcast.6, ...), custom_call_target="tpu_custom_call" | custom-call | tf_op jit(solution)/shard_map/exchange/pallas_call | solution.py:527
  62.8 4.8 %backward.1 = (bf16[69,48,128]{2,1,0:T(8,128)(2,1)}, bf16[256,48,128]{2,1,0:T(8,128)(2,1)}) custom-call(bf16[20,72,128]{2,1,0:T(8,128)(2,1)} %get-tuple-element.8.grad_in, bf16[256,768]{1,0:T(8,128)(2,1)} %get-tuple-element.9.wb_in, bf16[256,48,128]{2,1,0:T(8,128)(2,1)} %get-tuple-element.10.slope_in, bf16[69,48,128]{2,1,0:T(8,128)(2,1)} %get-tuple-element.11.pred_in), custom_call_target="tpu_custom_call" | custom-call | tf_op jit(solution)/shard_map/backward/pallas_call | solution.py:577
